TPU v7x, 32 devices: a whole 2x2x4 slice. The times are simulated.
32 devices in a mesh: dp: 2 (over x), ep: 16 (over z, y, core).
Axes of the slice: x: 2, y: 2, z: 4, core: 2. Of those that a mesh axis runs over, the one named last changes fastest.
Arguments:
- x0: bfloat16 [2048, 1024], P(('dp', 'ep')), parts along dimension 0
- idx_a: int32 [2048, 8], P(('dp', 'ep')), parts along dimension 0
- g_a: float32 [2048, 8], P(('dp', 'ep')), parts along dimension 0
- idx_b: int32 [2048, 8], P(('dp', 'ep')), parts along dimension 0
- g_b: float32 [2048, 8], P(('dp', 'ep')), parts along dimension 0
- dy: bfloat16 [2048, 1024], P(('dp', 'ep')), parts along dimension 0
- w1_a: bfloat16 [32, 1024, 512], P('ep')
- w3_a: bfloat16 [32, 1024, 512], P('ep')
- w2_a: bfloat16 [32, 512, 1024], P('ep')
- w1_b: bfloat16 [32, 1024, 512], P('ep')
- w3_b: bfloat16 [32, 1024, 512], P('ep')
- w2_b: bfloat16 [32, 512, 1024], P('ep')
Outputs:
- output 1: bfloat16 [2048, 1024], P(('dp', 'ep')), parts along dimension 0
- output 2: bfloat16 [2048, 1024], P(('dp', 'ep')), parts along dimension 0
- output 3: float32 [64, 1024, 512], P(('dp', 'ep')), parts along dimension 0
- output 4: float32 [64, 1024, 512], P(('dp', 'ep')), parts along dimension 0
- output 5: float32 [64, 512, 1024], P(('dp', 'ep')), parts along dimension 0
- output 6: float32 [64, 1024, 512], P(('dp', 'ep')), parts along dimension 0
- output 7: float32 [64, 1024, 512], P(('dp', 'ep')), parts along dimension 0
- output 8: float32 [64, 512, 1024], P(('dp', 'ep')), parts along dimension 0
- output 9: float32 [2048, 8], P(('dp', 'ep')), parts along dimension 0
- output 10: float32 [2048, 8], P(('dp', 'ep')), parts along dimension 0
There are 2 independent parts. A program takes and returns all parts, laid end to end along the dimension named above; an argument that names none is the same for every part.
All inputs are finite; a program needn't handle non-finite values.
Results may differ from a plain program's by a relative error of at most 0.00872247.
Values are sent between devices in bfloat16 or wider.
A program may use at most 1 GiB of HBM per device.

v0:
```python
import jax
import jax.numpy as jnp
from jax import lax
from jax.sharding import PartitionSpec as P

F32 = jnp.float32
BF = jnp.bfloat16


def _gates(idx, g, n_exp, el):
    m = idx[:, :, None] == jnp.arange(n_exp)
    gm = jnp.max(jnp.where(m, g[:, :, None], -1.0), axis=1)
    gm = lax.all_gather(gm, 'ep', axis=0, tiled=True)
    i = lax.axis_index('ep')
    return lax.dynamic_slice_in_dim(gm, i * el, el, axis=1).T


def _hidden(u, w1, w3):
    a1 = jnp.einsum('rd,edf->erf', u, w1, preferred_element_type=F32)
    a3 = jnp.einsum('rd,edf->erf', u, w3, preferred_element_type=F32)
    sg = jax.nn.sigmoid(a1)
    sl = a1 * sg
    return a1, a3, sg, sl, (sl * a3).astype(BF)


def _forward(x, u, gc, w1, w3, w2):
    gc = gc[:, :, None]
    h = _hidden(u, w1, w3)[4]
    o = jnp.einsum('erf,efd->erd', h, w2, preferred_element_type=F32).astype(BF)
    y = jnp.sum(jnp.where(gc >= 0, gc * o.astype(F32), 0.0), axis=0)
    y = lax.psum_scatter(y, 'ep', scatter_dimension=0, tiled=True)
    return (x.astype(F32) + y).astype(BF)


def _backward(u, z, zb, idx, gc, w1, w3, w2):
    el = w1.shape[0]
    gc = gc[:, :, None]
    ok = gc >= 0
    a1, a3, sg, sl, h = _hidden(u, w1, w3)
    h = jnp.where(ok, h, jnp.zeros_like(h))
    r = jnp.einsum('rd,efd->erf', zb, w2, preferred_element_type=F32)
    dg = jnp.sum(jnp.where(ok, h.astype(F32) * r, 0.0), axis=2)
    do = jnp.where(ok, gc * zb.astype(F32)[None], 0.0).astype(BF)
    dw2 = jnp.einsum('erf,erd->efd', h, do, preferred_element_type=F32)
    dh = gc * r
    da3 = jnp.where(ok, dh * sl, 0.0).astype(BF)
    da1 = jnp.where(ok, dh * a3 * sg * (1.0 + a1 * (1.0 - sg)), 0.0).astype(BF)
    dw1 = jnp.einsum('rd,erf->edf', u, da1, preferred_element_type=F32)
    dw3 = jnp.einsum('rd,erf->edf', u, da3, preferred_element_type=F32)
    du = (jnp.einsum('erf,edf->erd', da1, w1, preferred_element_type=F32)
          + jnp.einsum('erf,edf->erd', da3, w3, preferred_element_type=F32)).astype(BF)
    du = lax.psum_scatter(jnp.sum(du.astype(F32), axis=0), 'ep', scatter_dimension=0, tiled=True)
    dx = (z.astype(F32) + du).astype(BF)
    t = z.shape[0]
    dg = lax.all_to_all(dg.reshape(el, -1, t), 'ep', 1, 0, tiled=True)
    dg = dg.reshape(-1, t)
    dgt = jnp.sum(jnp.where(idx[:, :, None] == jnp.arange(dg.shape[0]), dg.T[:, None, :], 0.0), axis=2)
    return dx, dw1, dw3, dw2, dgt


def solution(mesh):
    tok = P(('dp', 'ep'))
    wsp = P('ep')
    c = mesh.shape['ep']

    def body(x0, idx_a, g_a, idx_b, g_b, dy, w1_a, w3_a, w2_a, w1_b, w3_b, w2_b):
        el = w1_a.shape[0]
        ga = _gates(idx_a, g_a, el * c, el)
        gb = _gates(idx_b, g_b, el * c, el)
        ag = lambda v: lax.all_gather(v, 'ep', axis=0, tiled=True)
        u0 = ag(x0)
        zb = ag(dy)
        x1 = _forward(x0, u0, ga, w1_a, w3_a, w2_a)
        u1 = ag(x1)
        x2 = _forward(x1, u1, gb, w1_b, w3_b, w2_b)
        dx1, dw1_b, dw3_b, dw2_b, dg_b = _backward(u1, dy, zb, idx_b, gb, w1_b, w3_b, w2_b)
        dx0, dw1_a, dw3_a, dw2_a, dg_a = _backward(u0, dx1, ag(dx1), idx_a, ga, w1_a, w3_a, w2_a)
        return x2, dx0, dw1_a, dw3_a, dw2_a, dw1_b, dw3_b, dw2_b, dg_a, dg_b

    return jax.shard_map(body, mesh=mesh,
                         in_specs=(tok,) * 6 + (wsp,) * 6,
                         out_specs=(tok,) * 10,
                         check_vma=False)
```

profile of v0, /device:TPU:0, one launch (start us, length us, event | category | flops | bytes accessed | tf_op | source)
XLA Modules:
  0.0 521.3 jit_solution(12142547939881449607)
XLA Ops:
  8.7 24.0 %all-gather = f32[16,64,32]{1,2,0:T(8,128)S(1)} all-gather(f32[1,64,32]{1,2,0:T(8,128)S(1)} %bitcast.188), channel_id=1, replica_groups=mesh['dp'=2,'ep'=16] {'ep'}, dimensions={0}, use_global_device_ids=true | all-gather | bytes 139264 | tf_op jit(solution)/shard_map/all_gather | solution.py:13
  33.1 21.7 %all-gather.7.cloned.1.call-done = bf16[1024,1024]{1,0:T(8,128)(2,1)} async-done(((bf16[64,1024]{1,0:T(8,128)(2,1)}), bf16[1024,1024]{1,0:T(8,128)(2,1)}) %all-gather.7.cloned.1.call-update) | async-done | bytes 2097168 | tf_op jit(solution)/shard_map/all_gather | solution.py:70
  54.8 4.7 fusion.46
  59.6 5.0 fusion.15
  65.9 5.1 select_reduce_fusion.1
  71.1 71.6 %reduce-scatter.5.cloned.1.call-done = f32[64,1024]{1,0:T(8,128)} async-done(((f32[1024,1024]{1,0:T(8,128)}), f32[64,1024]{1,0:T(8,128)}) %reduce-scatter.5.cloned.1.call-update) | async-done | bytes 262160 | tf_op jit(solution)/shard_map/reduce_scatter | solution.py:31
  145.0 20.5 %all-gather.1 = f32[16,64,32]{1,2,0:T(8,128)S(1)} all-gather(f32[1,64,32]{1,2,0:T(8,128)S(1)} %bitcast.189), channel_id=1, replica_groups=mesh['dp'=2,'ep'=16] {'ep'}, dimensions={0}, use_global_device_ids=true | all-gather | bytes 139264 | tf_op jit(solution)/shard_map/all_gather | solution.py:13
  165.7 20.7 %all-gather.9.cloned.1.call-done = bf16[1024,1024]{1,0:T(8,128)(2,1)} async-done(((bf16[64,1024]{1,0:T(8,128)(2,1)}), bf16[1024,1024]{1,0:T(8,128)(2,1)}) %all-gather.9.cloned.1.call-update) | async-done | bytes 2097168 | tf_op jit(solution)/shard_map/all_gather | solution.py:70
  186.5 6.8 %fusion.38 = f32[1024,2,512]{0,2,1:T(8,128)} fusion(bf16[2,1024,512]{2,1,0:T(8,128)(2,1)} %param.22, bf16[1024,1024]{1,0:T(8,128)(2,1)} %all-gather.9.cloned.1.call-done), kind=kOutput, calls=%fused_computation.66 | convolution fusion | flops 2147483648 | bytes 8388608 | tf_op jit(solution)/shard_map/rd,edf->erf/dot_general | solution.py:20
  197.7 31.1 %all-gather.11.cloned.1.call-done = bf16[1024,1024]{1,0:T(8,128)(2,1)} async-done(((bf16[64,1024]{1,0:T(8,128)(2,1)}), bf16[1024,1024]{1,0:T(8,128)(2,1)}) %all-gather.11.cloned.1.call-update) | async-done | bytes 2097168 | tf_op jit(solution)/shard_map/all_gather | solution.py:70
  228.7 9.0 %fusion.5 = (f32[2,1024]{1,0:T(2,128)S(1)}, bf16[2,1024,512]{1,2,0:T(8,128)(2,1)}, bf16[2,1024,512]{1,2,0:T(8,128)(2,1)S(1)}, bf16[2,1024,512]{1,2,0:T(8,128)(2,1)S(1)}) fusion(pred[2,1024]{1,0:T(4,128)(4,1)S(1)} %get-tuple-element.64, f32[1024,2,512]{0,2,1:T(8,128)} %fusion.38, f32[1024,2,512]{0,2,1:T(8,128)} %fusion.40, ...), kind=kOutput, calls=%fused_computation.17 | convolution fusion | flops 2171598848 | bytes 18892800 | tf_op jit(solution)/shard_map/rd,efd->erf/dot_general | solution.py:41
  240.9 5.3 %convert_reduce_fusion.1 = f32[1024,1024]{1,0:T(8,128)} fusion(f32[2,1024,1024]{2,1,0:T(8,128)S(1)} %fusion.55, bf16[2,1024,512]{1,2,0:T(8,128)(2,1)S(1)} %get-tuple-element.69, bf16[2,1024,512]{2,1,0:T(8,128)(2,1)S(1)} %copy-done.11), kind=kOutput, calls=%fused_computation.4 | convolution fusion | flops 2154823680 | bytes 16777216 | tf_op jit(solution)/shard_map/erf,edf->erd/dot_general | solution.py:51
  246.2 71.5 %reduce-scatter.9.cloned.1.call-done = f32[64,1024]{1,0:T(8,128)} async-done(((f32[1024,1024]{1,0:T(8,128)}), f32[64,1024]{1,0:T(8,128)}) %reduce-scatter.9.cloned.1.call-update) | async-done | bytes 262160 | tf_op jit(solution)/shard_map/reduce_scatter | solution.py:52
  319.4 6.9 %select_reduce_fusion = f32[1024,1024]{1,0:T(8,128)} fusion(f32[2,1024]{1,0:T(2,128)S(1)} %get-tuple-element.65, pred[2,1024]{1,0:T(4,128)(4,1)S(1)} %get-tuple-element.64, bf16[2,1024,512]{1,2,0:T(8,128)(2,1)} %get-tuple-element.61, bf16[2,512,1024]{2,1,0:T(8,128)(2,1)S(1)} %copy-done), kind=kOutput, calls=%fused_computation.6 | convolution fusion | flops 2156920832 | bytes 8398848 | tf_op jit(solution)/shard_map/erf,efd->erd/dot_general | solution.py:29
  326.6 34.0 %all-gather.13.cloned.1.call-done = bf16[1024,1024]{1,0:T(8,128)(2,1)} async-done(((bf16[64,1024]{1,0:T(8,128)(2,1)}), bf16[1024,1024]{1,0:T(8,128)(2,1)}) %all-gather.13.cloned.1.call-update) | async-done | bytes 2097168 | tf_op jit(solution)/shard_map/all_gather | solution.py:70
  360.6 9.9 %select_convert_fusion.4 = (bf16[2,1024,512]{1,2,0:T(8,128)(2,1)S(1)}, bf16[2,1024,512]{1,2,0:T(8,128)(2,1)S(1)}, f32[2,1024]{1,0:T(2,128)S(1)}) fusion(f32[2,1024]{1,0:T(2,128)S(1)} %get-tuple-element.63, pred[2,1024]{1,0:T(4,128)(4,1)S(1)} %get-tuple-element.62, f32[2,512,1024]{2,1,0:T(8,128)} %copy-done.33, f32[2,512,1024]{2,1,0:T(8,128)} %get-tuple-element.72, ...), kind=kOutput, calls=%fused_computation.48 | convolution fusion | flops 2169501696 | bytes 18892800 | tf_op jit(solution)/shard_map/rd,efd->erf/dot_general | solution.py:41
  373.6 5.2 convert_reduce_fusion
  387.4 6.7 %convolution_bitcast_fusion.1 = f32[2,1024,512]{1,2,0:T(8,128)} fusion(bf16[2,1024,512]{1,2,0:T(8,128)(2,1)} %copy-done.8, bf16[1024,1024]{1,0:T(8,128)(2,1)} %all-gather.9.cloned.1.call-done), kind=kOutput, calls=%fused_computation.57 | convolution fusion | flops 2147483648 | bytes 8388608 | tf_op jit(solution)/shard_map/rd,erf->edf/dot_general | solution.py:48
  402.7 5.4 %copy.124 = f32[2,1024,512]{2,1,0:T(8,128)} copy(f32[2,1024,512]{1,2,0:T(8,128)} %convolution_bitcast_fusion.1) | data formatting | bytes 8388608
  408.1 5.5 %copy.125 = f32[2,1024,512]{2,1,0:T(8,128)} copy(f32[2,1024,512]{1,2,0:T(8,128)} %convolution_bitcast_fusion) | data formatting | bytes 8388608
  415.5 21.0 %reduce-scatter.7.cloned.1.call-done = f32[64,1024]{1,0:T(8,128)} async-done(((f32[1024,1024]{1,0:T(8,128)}), f32[64,1024]{1,0:T(8,128)}) %reduce-scatter.7.cloned.1.call-update) | async-done | bytes 262160 | tf_op jit(solution)/shard_map/reduce_scatter | solution.py:31
  457.7 5.5 %copy.122 = f32[2,1024,512]{2,1,0:T(8,128)} copy(f32[2,1024,512]{1,2,0:T(8,128)} %convolution_bitcast_fusion.3) | data formatting | bytes 8388608
  463.3 5.4 %copy.123 = f32[2,1024,512]{2,1,0:T(8,128)} copy(f32[2,1024,512]{1,2,0:T(8,128)} %convolution_bitcast_fusion.2) | data formatting | bytes 8388608
  470.1 42.3 %reduce-scatter.11.cloned.1.call-done = f32[64,1024]{1,0:T(8,128)} async-done(((f32[1024,1024]{1,0:T(8,128)}), f32[64,1024]{1,0:T(8,128)}) %reduce-scatter.11.cloned.1.call-update) | async-done | bytes 262160 | tf_op jit(solution)/shard_map/reduce_scatter | solution.py:52
  (123 shorter events, 61.6 us)
Async XLA Ops:
  7.2 221.6 %copy-start = (bf16[2,512,1024]{2,1,0:T(8,128)(2,1)S(1)}, bf16[2,512,1024]{2,1,0:T(8,128)(2,1)}, u32[]{:S(2)}) copy-start(bf16[2,512,1024]{2,1,0:T(8,128)(2,1)} %param.23) | copy-start | bytes 6291460
  7.2 47.6 %all-gather.7.cloned.1.call-start = ((), (), s32[]{:S(2)}) async-start(), calls=%async_computation.6 | async-start | bytes 2228224 | tf_op jit(solution)/shard_map/all_gather | solution.py:70
  7.9 134.7 %reduce-scatter.5.cloned.1.call-start = ((), (), s32[]{:S(2)}) async-start(), calls=%async_computation.7 | async-start | bytes 4456448 | tf_op jit(solution)/shard_map/reduce_scatter | solution.py:31
  71.0 71.7 %copy-start.20 = (bf16[64,1024]{1,0:T(8,128)(2,1)S(1)}, bf16[64,1024]{1,0:T(8,128)(2,1)}, u32[]{:S(2)}) copy-start(bf16[64,1024]{1,0:T(8,128)(2,1)} %param.12) | copy-start | bytes 393220
  71.0 73.9 %copy-start.22 = (s32[64,8]{0,1:T(8,128)S(1)}, s32[64,8]{0,1:T(8,128)}, u32[]{:S(2)}) copy-start(s32[64,8]{0,1:T(8,128)} %param.15) | copy-start | bytes 6148
  71.0 73.9 %copy-start.24 = (f32[64,8]{0,1:T(8,128)S(1)}, f32[64,8]{0,1:T(8,128)}, u32[]{:S(2)}) copy-start(f32[64,8]{0,1:T(8,128)} %param.16) | copy-start | bytes 6148
  71.0 115.4 %all-gather.9.cloned.1.call-start = ((), (), s32[]{:S(2)}) async-start(), calls=%async_computation.8 | async-start | bytes 2228224 | tf_op jit(solution)/shard_map/all_gather | solution.py:70
  144.3 84.4 %all-gather.11.cloned.1.call-start = ((), (), s32[]{:S(2)}) async-start(), calls=%async_computation.10 | async-start | bytes 2228224 | tf_op jit(solution)/shard_map/all_gather | solution.py:70
  144.9 172.9 %reduce-scatter.9.cloned.1.call-start = ((), (), s32[]{:S(2)}) async-start(), calls=%async_computation.11 | async-start | bytes 4456448 | tf_op jit(solution)/shard_map/reduce_scatter | solution.py:52
  186.5 6.8 %copy-start.5 = (bf16[2,1024,512]{2,1,0:T(8,128)(2,1)S(1)}, bf16[2,1024,512]{2,1,0:T(8,128)(2,1)}, u32[]{:S(2)}) copy-start(bf16[2,1024,512]{2,1,0:T(8,128)(2,1)} %param.21) | copy-start | bytes 6291460
  186.5 6.8 %copy-start.28 = (bf16[1024,1024]{1,0:T(8,128)(2,1)S(1)}, bf16[1024,1024]{1,0:T(8,128)(2,1)}, u32[]{:S(2)}) copy-start(bf16[1024,1024]{1,0:T(8,128)(2,1)} %all-gather.9.cloned.1.call-done) | copy-start | bytes 6291460
  228.7 9.0 %copy-start.6 = (bf16[2,1024,512]{2,1,0:T(8,128)(2,1)S(1)}, bf16[2,1024,512]{2,1,0:T(8,128)(2,1)}, u32[]{:S(2)}) copy-start(bf16[2,1024,512]{2,1,0:T(8,128)(2,1)} %param.21) | copy-start | bytes 6291460
  246.1 71.6 %copy-start.21 = (bf16[64,1024]{1,0:T(8,128)(2,1)S(1)}, bf16[64,1024]{1,0:T(8,128)(2,1)}, u32[]{:S(2)}) copy-start(bf16[64,1024]{1,0:T(8,128)(2,1)} %param.17) | copy-start | bytes 393220
  246.1 114.4 %all-gather.13.cloned.1.call-start = ((), (), s32[]{:S(2)}) async-start(), calls=%async_computation.12 | async-start | bytes 2228224 | tf_op jit(solution)/shard_map/all_gather | solution.py:70
  319.4 117.1 %reduce-scatter.7.cloned.1.call-start = ((), (), s32[]{:S(2)}) async-start(), calls=%async_computation.9 | async-start | bytes 4456448 | tf_op jit(solution)/shard_map/reduce_scatter | solution.py:31
  326.3 186.0 %reduce-scatter.11.cloned.1.call-start = ((), (), s32[]{:S(2)}) async-start(), calls=%async_computation.13 | async-start | bytes 4456448 | tf_op jit(solution)/shard_map/reduce_scatter | solution.py:52
  360.6 10.0 %copy-start.7 = (bf16[2,1024,512]{2,1,0:T(8,128)(2,1)S(1)}, bf16[2,1024,512]{2,1,0:T(8,128)(2,1)}, u32[]{:S(2)}) copy-start(bf16[2,1024,512]{2,1,0:T(8,128)(2,1)} %param.18) | copy-start | bytes 6291460
  383.7 29.9 %all-to-all-start.1 = ((f32[16,1,128]{2,1,0:T(1,128)}), f32[16,1,128]{2,1,0:T(1,128)S(1)}, u32[]{:S(2)}, u32[]{:S(2)}) async-start(f32[16,1,128]{2,1,0:T(1,128)} %reshape.62), calls=%async_computation.5 | async-start | bytes 16384 | tf_op jit(solution)/shard_map/all_to_all | solution.py:55
  387.4 6.7 %copy-start.2 = (f32[1024,1024]{1,0:T(8,128)S(1)}, f32[1024,1024]{1,0:T(8,128)}, u32[]{:S(2)}) copy-start(f32[1024,1024]{1,0:T(8,128)} %convert_element_type.110) | copy-start | bytes 12582916
  408.1 28.4 %copy-start.18 = (bf16[64,1024]{1,0:T(8,128)(2,1)S(1)}, bf16[64,1024]{1,0:T(8,128)(2,1)}, u32[]{:S(2)}) copy-start(bf16[64,1024]{1,0:T(8,128)(2,1)} %add_convert_fusion.5) | copy-start | bytes 393220
  408.1 34.6 %copy-start.3 = (bf16[1024,1024]{1,0:T(8,128)(2,1)S(1)}, bf16[1024,1024]{1,0:T(8,128)(2,1)}, u32[]{:S(2)}) copy-start(bf16[1024,1024]{1,0:T(8,128)(2,1)} %all-gather.13.cloned.1.call-done) | copy-start | bytes 6291460
  438.9 29.8 %all-to-all-start = ((f32[16,1,128]{2,1,0:T(1,128)}), f32[16,1,128]{2,1,0:T(1,128)S(1)}, u32[]{:S(2)}, u32[]{:S(2)}) async-start(f32[16,1,128]{2,1,0:T(1,128)} %reshape.60), calls=%async_computation.4 | async-start | bytes 16384 | tf_op jit(solution)/shard_map/all_to_all | solution.py:55
  457.7 56.3 %copy-start.1 = (bf16[2,512,1024]{2,1,0:T(8,128)(2,1)S(1)}, bf16[2,512,1024]{2,1,0:T(8,128)(2,1)}, u32[]{:S(2)}) copy-start(bf16[2,512,1024]{2,1,0:T(8,128)(2,1)} %param.23) | copy-start | bytes 6291460
  463.3 49.1 %copy-start.19 = (bf16[64,1024]{1,0:T(8,128)(2,1)S(1)}, bf16[64,1024]{1,0:T(8,128)(2,1)}, u32[]{:S(2)}) copy-start(bf16[64,1024]{1,0:T(8,128)(2,1)} %add_convert_fusion.3) | copy-start | bytes 393220
  (20 other events, 74.9 us)
Sparse Core Ops, SparseCore 0:
  10.2 44.5 all-gather.6
  71.1 71.4 reduce-scatter.4
  145.4 41.0 all-gather.8
  188.5 40.2 all-gather.10
  246.3 71.4 reduce-scatter.8
  319.8 40.7 all-gather.12
  365.0 71.4 reduce-scatter.6
  440.3 71.9 reduce-scatter.10
where the time goes:
time: 528 us; the launch traced here: 521 us
  waiting for transfers between devices  315 us (60%)
  matrix products  95.8 us (18%)
  blocking collectives  44.5 us (8%)
  local copies, waits for them, and re-layouts  30 us (6%)
  between operations  14.9 us (3%)
  other arithmetic  12.8 us (2%)
  starting transfers between devices  8.03 us (2%)
    reduce_scatter x2, waiting for transfers between devices, _backward(): lax.psum_scatter(jnp.sum(du.astype(F32), axis=0), 'ep', scatter_dimension...  114 us
    all_gather x4, waiting for transfers between devices, body(): ag = lambda v: lax.all_gather(v, 'ep', axis=0, tiled=True)  108 us
    reduce_scatter x2, waiting for transfers between devices, _forward(): y = lax.psum_scatter(y, 'ep', scatter_dimension=0, tiled=True)  92.6 us
    all_gather x2, blocking collectives, _gates(): gm = lax.all_gather(gm, 'ep', axis=0, tiled=True)  44.5 us
    unnamed x78, local copies, waits for them, and re-layouts  29 us
    dot_general x2, matrix products, _backward(): r = jnp.einsum('rd,efd->erf', zb, w2, preferred_element_type=F32)  18.9 us
    dot_general x2, matrix products, _forward(): o = jnp.einsum('erf,efd->erd', h, w2, preferred_element_type=F32).astype(BF)  11.9 us
    dot_general x2, matrix products, _hidden(): a3 = jnp.einsum('rd,edf->erf', u, w3, preferred_element_type=F32)  11.7 us
  transfers between devices with their start and end apart: 10, of which 8 were waited for; matrix products, arithmetic and copies ran while one was open for 19% of the time, Pallas kernels for 0%

commit v1 on v0

v1 whole, which is shorter than its diff:
```python
import jax
import jax.numpy as jnp
from jax import lax
from jax.experimental import pallas as pl
from jax.experimental.pallas import tpu as pltpu
from jax.sharding import PartitionSpec as P

F32 = jnp.float32
BF = jnp.bfloat16
MESH = pl.DeviceIdType.MESH
VMEM_LIMIT = 67043328

REL = (4, 3, -3, 2, -2, 1, -1, 0)
UP = (0, 1, 3, 5, 7)
DOWN = (0, 2, 4, 6, 7)


def _ring_pos(ep):
    z, y = ep // 4, (ep // 2) % 2
    return z + y * (7 - 2 * z)


def _ring_ep(pos, core):
    y = pos // 4
    z = pos + y * (7 - 2 * pos)
    return z * 4 + y * 2 + core


def _nt(a, b):
    return lax.dot_general(a, b, (((1,), (1,)), ((), ())), preferred_element_type=F32)


def _nn(a, b):
    return jnp.dot(a, b, preferred_element_type=F32)


def _main_kernel(x0_ref, dy_ref, gt_ref, w1a_h, w3a_h, w2a_h, w1b_h, w3b_h, w2b_h,
                 x2_ref, dx0_ref, dgr_ref, gc_ref, xg_o, zg_o, h_o, da1_o, da3_o,
                 w1, w3, w2, xg, ps, dr, ru, rd, a1s, a3s, hs, d1s, d3s, gtr, dgc, dgs,
                 wsem, ag_s, ag_r, ax_s, ax_r, rs_s, rs_r, rx_s, rx_r, g_s, g_r, d_s, d_r, osem):
    T = x0_ref.shape[0]
    H = T // 2
    me = lax.axis_index('ep')
    core = me % 2
    pos = _ring_pos(me)
    up = _ring_ep((pos + 1) % 8, core)
    down = _ring_ep((pos + 7) % 8, core)
    mate = me + 1 - 2 * core

    wcopies = []
    for l, refs in enumerate(((w1a_h, w3a_h, w2a_h), (w1b_h, w3b_h, w2b_h))):
        for i, (src, dst) in enumerate(zip(refs, (w1, w3, w2))):
            c = pltpu.make_async_copy(src, dst.at[l], wsem.at[l * 3 + i])
            c.start()
            wcopies.append(c)

    bar = pltpu.get_barrier_semaphore()
    for i in range(1, 16):
        pl.semaphore_signal(bar, inc=1, device_id={'ep': (me + i) % 16}, device_id_type=MESH)
    pl.semaphore_wait(bar, 15)

    def rcopy(src, dst, ss, rs, dev):
        return pltpu.make_async_remote_copy(src_ref=src, dst_ref=dst, send_sem=ss, recv_sem=rs,
                                            device_id={'ep': dev}, device_id_type=MESH)

    def half(i):
        return pl.ds(i * H, H)

    pending = []

    def ag_msgs(n):
        buf = xg.at[n]
        u, d, m = [], [], []
        usl, dsl = (7, 6, 4, 2, 0), (7, 5, 3, 1, 0)
        for j in range(7):
            hu, hd = j % 2, 1 - j % 2
            u.append(rcopy(buf.at[usl[j // 2], 0, half(hu)], buf.at[usl[j // 2 + 1], 0, half(hu)],
                           ag_s.at[n, 0, j], ag_r.at[n, 0, j], up))
            d.append(rcopy(buf.at[dsl[j // 2], 0, half(hd)], buf.at[dsl[j // 2 + 1], 0, half(hd)],
                           ag_s.at[n, 1, j], ag_r.at[n, 1, j], down))
        for k in range(8):
            for hf in range(2):
                m.append(rcopy(buf.at[k, 0, half(hf)], buf.at[k, 1, half(hf)],
                               ax_s.at[n, k * 2 + hf], ax_r.at[n, k * 2 + hf], mate))
        return u, d, m

    def ag_start(n):
        u, d, m = ag_msgs(n)
        for j in range(2):
            u[j].start()
            d[j].start()
        for hf in range(2):
            m[7 * 2 + hf].start()
        return u, d, m

    def ag_finish(msgs):
        u, d, m = msgs
        usl, dsl = (6, 4, 2, 0), (5, 3, 1, 0)
        for j in range(7):
            u[j].wait_recv()
            if j + 2 < 7:
                u[j + 2].start()
            m[usl[j // 2] * 2 + j % 2].start()
            d[j].wait_recv()
            if j + 2 < 7:
                d[j + 2].start()
            m[dsl[j // 2] * 2 + 1 - j % 2].start()
        for c in m:
            c.wait_recv()
        pending.extend(u + d + m)

    def rs_local_msgs(n, b):
        return [rcopy(ps.at[b, pl.ds(2 * ch, 2), 1], dr.at[b, pl.ds(2 * ch, 2)],
                      rx_s.at[n, ch], rx_r.at[n, ch], mate) for ch in range(4)]

    def rs_msgs(n, b):
        u, d = [], []
        for j in range(7):
            k = (j + 1) // 2
            hu, hd = j % 2, 1 - j % 2
            u.append(rcopy(ps.at[b, UP[k], 0, half(hu)], ru.at[b, j], rs_s.at[n, 0, j], rs_r.at[n, 0, j], up))
            d.append(rcopy(ps.at[b, DOWN[k], 0, half(hd)], rd.at[b, j], rs_s.at[n, 1, j], rs_r.at[n, 1, j], down))
        return u, d

    def rs_run(n, b, loc):
        u, d = rs_msgs(n, b)

        def merge(ch):
            loc[ch].wait_recv()
            for k in (2 * ch, 2 * ch + 1):
                ps[b, k, 0] += dr[b, k]
        merge(0)
        u[0].start()
        d[0].start()
        u[1].start()
        merge(1)
        d[1].start()
        merge(2)
        merge(3)
        for j in range(7):
            k = (j + 3) // 2
            hu, hd = j % 2, 1 - j % 2
            u[j].wait_recv()
            ps[b, UP[k], 0, half(hu)] += ru[b, j]
            if j + 2 < 7:
                u[j + 2].start()
            d[j].wait_recv()
            ps[b, DOWN[k], 0, half(hd)] += rd[b, j]
            if j + 2 < 7:
                d[j + 2].start()
        pending.extend(u + d + loc)

    def drain():
        for c in pending:
            c.wait_send()
        pending.clear()

    xg[0, 7, 0] = x0_ref[...]
    xg[1, 7, 0] = dy_ref[...]
    msgs0 = ag_start(0)
    gmsgs = []
    for k in range(8):
        q = (pos - REL[k] + 8) % 8
        for plane in range(2):
            if k == 7 and plane == 0:
                continue
            dev = _ring_ep(q, core + plane * (1 - 2 * core))
            c = rcopy(gt_ref.at[pl.ds(dev * 8, 8)], gtr.at[pl.ds((k * 2 + plane) * 8, 8)],
                      g_s.at[k * 2 + plane], g_r.at[k * 2 + plane], dev)
            c.start()
            gmsgs.append(c)
    gtr[14 * 8:15 * 8] = gt_ref[pl.ds(pl.multiple_of(me * 8, 8), 8)]
    ag_finish(msgs0)
    msgs1 = ag_start(1)
    for c in gmsgs:
        c.wait_recv()
    pending.extend(gmsgs)
    gct = gtr[...].T
    for b in range(16):
        gc_ref[b * T:(b + 1) * T, 0:8] = gct[0:T, b * 8:b * 8 + 8]

    R = 4 * T

    def hidden(n, l, e, rows, mask):
        u = rows_of(n, rows)
        a1 = _nn(u, w1[l, e])
        a3 = _nn(u, w3[l, e])
        sg = 1.0 / (1.0 + jnp.exp(-a1))
        sl = a1 * sg
        h = jnp.where(mask, sl * a3, 0.0).astype(BF)
        return a1, a3, sg, sl, h

    def rows_of(n, ch):
        return xg[n, pl.ds(2 * ch, 2)].reshape(R, -1)

    def put(b, ch, e, v):
        v = v.reshape(2, 2, T, v.shape[-1])
        if e == 0:
            ps[b, pl.ds(2 * ch, 2)] = v
        else:
            ps[b, pl.ds(2 * ch, 2)] += v

    def rowslice(ch):
        return pl.ds(pl.multiple_of(ch * R, R), R)

    for c in wcopies[:3]:
        c.wait()
    loc = rs_local_msgs(0, 0)

    @pl.loop(0, 4)
    def _(ch):
        rows = rowslice(ch)
        for e in range(2):
            g = gc_ref[rows, e:e + 1]
            a1, a3, sg, sl, h = hidden(0, 0, e, ch, g >= 0)
            a1s[e, rows] = a1
            a3s[e, rows] = a3
            o = _nn(h, w2[0, e]).astype(BF).astype(F32)
            put(0, ch, e, g * o)
    for c in loc:
        c.start()
    ag_finish(msgs1)
    rs_run(0, 0, loc)
    xg[2, 7, 0] = (x0_ref[...].astype(F32) + ps[0, 7, 0]).astype(BF)
    ag_finish(ag_start(2))
    drain()

    def back(l, nz, b, ch, rows, e, g, a1, a3, sg, sl, h):
        mask = g >= 0
        r = _nt(rows_of(nz, ch), w2[l, e])
        dgc[rows, 2 * l + e:2 * l + e + 1] = jnp.sum(h.astype(F32) * r, axis=1, keepdims=True)
        dh = g * r
        da3 = jnp.where(mask, dh * sl, 0.0).astype(BF)
        da1 = jnp.where(mask, dh * a3 * sg * (1.0 + a1 * (1.0 - sg)), 0.0).astype(BF)
        hs[l, e, rows] = h
        d1s[l, e, rows] = da1
        d3s[l, e, rows] = da3
        du = (_nt(da1, w1[l, e]) + _nt(da3, w3[l, e])).astype(BF).astype(F32)
        put(b, ch, e, du)

    for c in wcopies[3:]:
        c.wait()
    locx = rs_local_msgs(1, 1)
    loc = rs_local_msgs(2, 0)

    @pl.loop(0, 4)
    def _(ch):
        rows = rowslice(ch)
        for e in range(2):
            g = gc_ref[rows, 2 + e:3 + e]
            a1, a3, sg, sl, h = hidden(2, 1, e, ch, g >= 0)
            o = _nn(h, w2[1, e]).astype(BF).astype(F32)
            put(1, ch, e, g * o)
            back(1, 1, 0, ch, rows, e, g, a1, a3, sg, sl, h)
    for c in loc + locx:
        c.start()
    outs = []

    def out(src, dst, i):
        c = pltpu.make_async_copy(src, dst, osem.at[i])
        c.start()
        outs.append(c)
    for i, (s, d) in enumerate(((hs, h_o), (d1s, da1_o), (d3s, da3_o))):
        out(s.at[1], d.at[1], i)
    out(xg.at[0], xg_o.at[0], 3)
    out(xg.at[2], xg_o.at[1], 4)
    out(xg.at[1], zg_o.at[1], 5)
    rs_run(2, 0, loc)
    xg[3, 7, 0] = (dy_ref[...].astype(F32) + ps[0, 7, 0]).astype(BF)
    m3 = ag_start(3)
    ag_finish(m3)
    drain()
    out(xg.at[3], zg_o.at[0], 6)

    loc = rs_local_msgs(3, 0)

    @pl.loop(0, 4)
    def _(ch):
        rows = rowslice(ch)
        for e in range(2):
            g = gc_ref[rows, e:e + 1]
            a1 = a1s[e, rows]
            a3 = a3s[e, rows]
            sg = 1.0 / (1.0 + jnp.exp(-a1))
            sl = a1 * sg
            h = jnp.where(g >= 0, sl * a3, 0.0).astype(BF)
            back(0, 3, 0, ch, rows, e, g, a1, a3, sg, sl, h)
    for c in loc:
        c.start()
    for i, (s, d) in enumerate(((hs, h_o), (d1s, da1_o), (d3s, da3_o))):
        out(s.at[0], d.at[0], 7 + i)

    dmsgs = []
    for k in range(8):
        t = dgc[k * 2 * T:(k + 1) * 2 * T].T[0:8]
        dgs[k * 16:k * 16 + 8] = t
        dgs[k * 16 + 8:k * 16 + 16] = pltpu.roll(t, T, 1)
        q = (pos + REL[k] + 8) % 8
        for plane in range(2):
            b = k * 2 + plane
            if k == 7 and plane == 0:
                continue
            dev = _ring_ep(q, core + plane * (1 - 2 * core))
            c = rcopy(dgs.at[pl.ds(b * 8, 8)], dgr_ref.at[pl.ds(me * 8, 8)], d_s.at[b], d_r.at[b], dev)
            c.start()
            dmsgs.append(c)
    dgr_ref[pl.ds(pl.multiple_of(me * 8, 8), 8)] = dgs[14 * 8:15 * 8]

    rs_run(1, 1, locx)
    x2_ref[...] = (xg[2, 7, 0].astype(F32) + ps[1, 7, 0]).astype(BF)
    rs_run(3, 0, loc)
    dx0_ref[...] = (xg[3, 7, 0].astype(F32) + ps[0, 7, 0]).astype(BF)
    for c in dmsgs:
        c.wait_recv()
    pending.extend(dmsgs)
    drain()
    for c in outs:
        c.wait()


def _main(x0, dy, gt, ws):
    T, D = x0.shape
    EL, _, F = ws[0].shape
    N = 16 * T
    S = jax.ShapeDtypeStruct
    vm = pl.BlockSpec(memory_space=pltpu.VMEM)
    hb = pl.BlockSpec(memory_space=pl.ANY)
    dma = pltpu.SemaphoreType.DMA
    return pl.pallas_call(
        _main_kernel,
        out_shape=(S((T, D), BF), S((T, D), BF), S((128, 128), F32), S((N, 128), F32),
                   S((2, 8, 2, T, D), BF), S((2, 8, 2, T, D), BF),
                   S((2, EL, N, F), BF), S((2, EL, N, F), BF), S((2, EL, N, F), BF)),
        in_specs=[vm] * 3 + [hb] * 6,
        out_specs=(vm, vm, vm, vm) + (hb,) * 5,
        scratch_shapes=[
            pltpu.VMEM((2, EL, D, F), BF), pltpu.VMEM((2, EL, D, F), BF), pltpu.VMEM((2, EL, F, D), BF),
            pltpu.VMEM((4, 8, 2, T, D), BF),
            pltpu.VMEM((2, 8, 2, T, D), F32), pltpu.VMEM((2, 8, T, D), F32),
            pltpu.VMEM((2, 7, T // 2, D), F32), pltpu.VMEM((2, 7, T // 2, D), F32),
            pltpu.VMEM((EL, N, F), F32), pltpu.VMEM((EL, N, F), F32),
            pltpu.VMEM((2, EL, N, F), BF), pltpu.VMEM((2, EL, N, F), BF), pltpu.VMEM((2, EL, N, F), BF),
            pltpu.VMEM((128, 128), F32), pltpu.VMEM((N, 128), F32), pltpu.VMEM((128, 128), F32),
            dma((6,)), dma((4, 2, 7)), dma((4, 2, 7)), dma((4, 16)), dma((4, 16)),
            dma((4, 2, 7)), dma((4, 2, 7)), dma((4, 4)), dma((4, 4)),
            dma((16,)), dma((16,)), dma((16,)), dma((16,)), dma((10,)),
        ],
        compiler_params=pltpu.CompilerParams(collective_id=0, has_side_effects=True,
                                             vmem_limit_bytes=VMEM_LIMIT),
        name='moe',
    )(x0, dy, gt, *ws)


def _tn(a, b):
    return lax.dot_general(a, b, (((0,), (0,)), ((), ())), preferred_element_type=F32)


def _wgrad_kernel(l, xg, zg, gc, h, d1, d3, o1, o3, o2):
    e = pl.program_id(0)
    x = xg[0]
    o1[0] = _tn(x, d1[0, 0])
    o3[0] = _tn(x, d3[0, 0])
    g = jnp.where(e == 0, gc[:, 2 * l:2 * l + 1], gc[:, 2 * l + 1:2 * l + 2])
    do = jnp.where(g >= 0, g * zg[0].astype(F32), 0.0).astype(BF)
    o2[0] = _tn(h[0, 0], do)


def _wgrad(l, xg, zg, gc, h, d1, d3):
    import functools
    _, N, D = xg.shape
    EL, F = h.shape[1], h.shape[3]
    S = jax.ShapeDtypeStruct
    tok = pl.BlockSpec((1, N, D), lambda e: (l, 0, 0))
    act = pl.BlockSpec((1, 1, N, F), lambda e: (l, e, 0, 0))
    return pl.pallas_call(
        functools.partial(_wgrad_kernel, l),
        grid=(EL,),
        out_shape=(S((EL, D, F), F32), S((EL, D, F), F32), S((EL, F, D), F32)),
        in_specs=[tok, tok, pl.BlockSpec((N, 128), lambda e: (0, 0)), act, act, act],
        out_specs=(pl.BlockSpec((1, D, F), lambda e: (e, 0, 0)),) * 2 + (pl.BlockSpec((1, F, D), lambda e: (e, 0, 0)),),
        compiler_params=pltpu.CompilerParams(vmem_limit_bytes=VMEM_LIMIT),
        name='wgrad',
    )(xg, zg, gc, h, d1, d3)


def solution(mesh):
    tok = P(('dp', 'ep'))
    wsp = P('ep')

    def gates(idx, g, ne):
        m = idx[:, :, None] == jnp.arange(ne)
        return jnp.max(jnp.where(m, g[:, :, None], -1.0), axis=1)

    def body(x0, idx_a, g_a, idx_b, g_b, dy, *ws):
        T, D = x0.shape
        EL = ws[0].shape[0]
        ne = 16 * EL
        ga = gates(idx_a, g_a, ne).T.reshape(16, EL, T)
        gb = gates(idx_b, g_b, ne).T.reshape(16, EL, T)
        gt = jnp.concatenate([ga, gb], axis=1)
        gt = jnp.pad(gt, ((0, 0), (0, 8 - 2 * EL), (0, 128 - T)), constant_values=-1.0).reshape(128, 128)
        x2, dx0, dgr, gc, xg, zg, h, d1, d3 = _main(x0, dy, gt, ws)
        N = 16 * T
        xg = xg.reshape(2, N, D)
        zg = zg.reshape(2, N, D)
        dwb = _wgrad(1, xg, zg, gc, h, d1, d3)
        dwa = _wgrad(0, xg, zg, gc, h, d1, d3)

        dgr = dgr.reshape(16, 8, 128)[:, :, :T]

        def dgate(l, idx):
            d = dgr[:, l * EL:(l + 1) * EL].reshape(ne, T).T
            return jnp.sum(jnp.where(idx[:, :, None] == jnp.arange(ne), d[:, None, :], 0.0), axis=2)
        return (x2, dx0) + tuple(dwa) + tuple(dwb) + (dgate(0, idx_a), dgate(1, idx_b))

    return jax.shard_map(body, mesh=mesh,
                         in_specs=(tok,) * 6 + (wsp,) * 6,
                         out_specs=(tok,) * 10,
                         check_vma=False)
```

time: 528 us -> 228 us (0.43); the launches traced: 521 us -> 228 us
  waiting for transfers between devices: 315 us -> 0 us
  Pallas kernels: 0 us -> 219 us
  matrix products: 95.8 us -> 0 us
  blocking collectives: 44.5 us -> 0 us
  local copies, waits for them, and re-layouts: 30 us -> 4.06 us
  between operations: 14.9 us -> 0.66 us
  other arithmetic: 12.8 us -> 3.47 us
  starting transfers between devices: 8.03 us -> 0 us
    pallas_call x0 -> x3, Pallas kernels: none -> 219 us  [the longest x1 195 us: _main(): pl.pallas_call(_main_kernel, out_shape=(S((T, D), BF), S((T, D), BF), S((...]
    reduce_scatter x4 -> x0, waiting for transfers between devices: 206 us -> none  [the longest x2 114 us: _backward(): lax.psum_scatter(jnp.sum(du.astype(F32), axis=0), 'ep', scatter_dimension...]
    all_gather x4 -> x0, waiting for transfers between devices: 108 us -> none  [body(): ag = lambda v: lax.all_gather(v, 'ep', axis=0, tiled=True)]
    dot_general x18 -> x0, matrix products: 95.8 us -> none  [the longest x2 18.9 us: _backward(): r = jnp.einsum('rd,efd->erf', zb, w2, preferred_element_type=F32)]
    all_gather x2 -> x0, blocking collectives: 44.5 us -> none  [_gates(): gm = lax.all_gather(gm, 'ep', axis=0, tiled=True)]
    unnamed x78 -> x2, local copies, waits for them, and re-layouts: 29 us -> 3.13 us
    convert_element_type x6 -> x0, other arithmetic: 9.44 us -> none  [the longest x2 3.26 us: _forward(): return (x.astype(F32) + y).astype(BF)]
    all_to_all x2 -> x0, starting transfers between devices: 7.49 us -> none  [_backward(): dg = lax.all_to_all(dg.reshape(el, -1, t), 'ep', 1, 0, tiled=True)]
  transfers between devices with their start and end apart: 10 -> 0, of which waited for: 8 -> 0; matrix products, arithmetic and copies ran while one was open for 19% -> 0% of each run, Pallas kernels for 0% -> 0%
where the time goes in v1:
time: 228 us
  Pallas kernels  219 us (96%)
  local copies, waits for them, and re-layouts  4.06 us (2%)
  other arithmetic  3.47 us (2%)
    pallas_call x1, Pallas kernels, _main(): pl.pallas_call(_main_kernel, out_shape=(S((T, D), BF), S((T, D), BF), S((...  195 us
    pallas_call x2, Pallas kernels, _wgrad(): pl.pallas_call(functools.partial(_wgrad_kernel, l), grid=(EL,), out_shape...  24.2 us

profile of v1, /device:TPU:0, one launch (start us, length us, event | category | flops | bytes accessed | tf_op | source)
XLA Modules:
  0.0 227.7 jit_solution(5592204593164880288)
XLA Ops:
  0.6 0.7 select_reduce_fusion.3
  1.4 0.7 select_reduce_fusion.2
  2.1 0.7 fusion.gt_ref
  2.8 195.2 %moe.1 = (bf16[64,1024]{1,0:T(8,128)(2,1)}, bf16[64,1024]{1,0:T(8,128)(2,1)}, f32[128,128]{1,0:T(8,128)}, f32[1024,128]{1,0:T(8,128)}, bf16[2,8,2,64,1024]{4,3,2...) custom-call(bf16[64,1024]{1,0:T(8,128)(2,1)} %x0_ref.1, ...), custom_call_target="tpu_custom_call" | custom-call | tf_op jit(solution)/shard_map/moe/pallas_call | solution.py:329
  198.0 0.9 fusion.1
  199.0 1.4 select_reduce_fusion
  200.3 12.1 %wgrad.3 = (f32[2,1024,512]{2,1,0:T(8,128)}, f32[2,1024,512]{2,1,0:T(8,128)}, f32[2,512,1024]{2,1,0:T(8,128)}) custom-call(bf16[2,1024,1024]{2,1,0:T(8,128)(2,1)} %bitcast.17, bf16[2,1024,1024]{2,1,0:T(8,128)(2,1)} %bitcast.19, f32[1024,128]{1,0:T(8,128)} %get-tuple-element.29.gc, bf16[2,2,1024,512]{3,2,1,0:T(8,128)(2,1)} %get-tuple-element.30.h, ...), custom_call_target="tpu_custom_call" | custom-call | tf_op jit(solution)/shard_map/wgrad/pallas_call | solution.py:375
  212.4 12.1 %wgrad.2 = (f32[2,1024,512]{2,1,0:T(8,128)}, f32[2,1024,512]{2,1,0:T(8,128)}, f32[2,512,1024]{2,1,0:T(8,128)}) custom-call(bf16[2,1024,1024]{2,1,0:T(8,128)(2,1)} %bitcast.18, bf16[2,1024,1024]{2,1,0:T(8,128)(2,1)} %bitcast.20, f32[1024,128]{1,0:T(8,128)} %get-tuple-element.29.gc, bf16[2,2,1024,512]{3,2,1,0:T(8,128)(2,1)} %get-tuple-element.30.h, ...), custom_call_target="tpu_custom_call" | custom-call | tf_op jit(solution)/shard_map/wgrad/pallas_call | solution.py:375
  224.5 1.6 copy.30
  226.1 1.6 copy.31

commit v2 on v0

v2 whole, which is shorter than its diff:
```python
import jax
import jax.numpy as jnp
from jax import lax
from jax.experimental import pallas as pl
from jax.experimental.pallas import tpu as pltpu
from jax.sharding import PartitionSpec as P

F32 = jnp.float32
BF = jnp.bfloat16
MESH = pl.DeviceIdType.MESH
VMEM_LIMIT = 67043328

REL = (-1, 0, -2, 1, 4, 3, -3, 2)
OWN = 1
UP = (4, 5, 7, 3, 1)
DOWN = (4, 6, 2, 0, 1)


def _ring_pos(ep):
    z, y = ep // 4, (ep // 2) % 2
    return z + y * (7 - 2 * z)


def _ring_ep(pos, core):
    y = pos // 4
    z = pos + y * (7 - 2 * pos)
    return z * 4 + y * 2 + core


def _nt(a, b):
    return lax.dot_general(a, b, (((1,), (1,)), ((), ())), preferred_element_type=F32)


def _nn(a, b):
    return jnp.dot(a, b, preferred_element_type=F32)


def _main_kernel(x0_ref, dy_ref, meta_ref, w1a_h, w3a_h, w2a_h, w1b_h, w3b_h, w2b_h,
                 x2_ref, dx0_ref, dgr_ref, gc_ref, xg_o, zg_o, h_o, da1_o, da3_o,
                 w1, w3, w2, xg, ps, dr, ru, rd, a1s, a3s, hs, d1s, d3s, gts, gtr, dgc, dgs, tmp1, tmp3,
                 wsem, ag_s, ag_r, ax_s, ax_r, rs_s, rs_r, rx_s, rx_r, g_s, g_r, d_s, d_r, osem):
    T = x0_ref.shape[0]
    H = T // 2
    R = 4 * T
    me = lax.axis_index('ep')
    core = me % 2
    pos = _ring_pos(me)
    up = _ring_ep((pos + 1) % 8, core)
    down = _ring_ep((pos + 7) % 8, core)
    mate = me + 1 - 2 * core

    wcopies = []
    for l, refs in enumerate(((w1a_h, w3a_h, w2a_h), (w1b_h, w3b_h, w2b_h))):
        for i, (src, dst) in enumerate(zip(refs, (w1, w3, w2))):
            c = pltpu.make_async_copy(src, dst.at[l], wsem.at[l * 3 + i])
            c.start()
            wcopies.append(c)

    bar = pltpu.get_barrier_semaphore()
    for i in range(1, 16):
        pl.semaphore_signal(bar, inc=1, device_id={'ep': (me + i) % 16}, device_id_type=MESH)
    xg[0, OWN, 0] = x0_ref[...]
    xg[1, OWN, 0] = dy_ref[...]
    for l in range(2):
        idx = meta_ref[8 * l:8 * l + 8]
        gate = meta_ref[16 + 8 * l:24 + 8 * l]
        for i in range(16):
            for e in range(2):
                row = jnp.max(jnp.where(idx == float(2 * i + e), gate, -1.0), axis=0, keepdims=True)
                gts[8 * i + 2 * l + e:8 * i + 2 * l + e + 1] = row
    for i in range(16):
        gts[8 * i + 4:8 * i + 8] = jnp.full((4, 128), -1.0, F32)
    dgc[...] = jnp.zeros_like(dgc)
    pl.semaphore_wait(bar, 15)

    def rcopy(src, dst, ss, rs, dev):
        return pltpu.make_async_remote_copy(src_ref=src, dst_ref=dst, send_sem=ss, recv_sem=rs,
                                            device_id={'ep': dev}, device_id_type=MESH)

    def half(i):
        return pl.ds(i * H, H)

    pending = []

    AU, AD = (1, 0, 2, 6, 4), (1, 3, 7, 5, 4)

    def ag_u(n, j):
        i, h = j // 2, half(j % 2)
        return rcopy(xg.at[n, AU[i], 0, h], xg.at[n, AU[i + 1], 0, h], ag_s.at[n, 0, j], ag_r.at[n, 0, j], up)

    def ag_d(n, j):
        i, h = j // 2, half(1 - j % 2)
        return rcopy(xg.at[n, AD[i], 0, h], xg.at[n, AD[i + 1], 0, h], ag_s.at[n, 1, j], ag_r.at[n, 1, j], down)

    def ag_m(n, k, hf):
        return rcopy(xg.at[n, k, 0, half(hf)], xg.at[n, k, 1, half(hf)],
                     ax_s.at[n, k * 2 + hf], ax_r.at[n, k * 2 + hf], mate)

    def ag_start(n):
        for j in range(2):
            ag_u(n, j).start()
            ag_d(n, j).start()
        for hf in range(2):
            ag_m(n, OWN, hf).start()

    def ag_step(n, *js):
        def f():
            for j in js:
                ag_u(n, j).wait_recv()
                if j + 2 < 7:
                    ag_u(n, j + 2).start()
                ag_d(n, j).wait_recv()
                if j + 2 < 7:
                    ag_d(n, j + 2).start()
                ag_m(n, AU[j // 2 + 1], j % 2).start()
                ag_m(n, AD[j // 2 + 1], 1 - j % 2).start()
        return f

    def ag_have(n, *ks):
        def f():
            for k in ks:
                for hf in range(2):
                    ag_m(n, k, hf).wait_recv()
        return f

    def ag_sent(n):
        for j in range(7):
            ag_u(n, j).wait_send()
            ag_d(n, j).wait_send()
        for k in range(8):
            for hf in range(2):
                ag_m(n, k, hf).wait_send()

    def rs_l(n, b, ch):
        return rcopy(ps.at[b, pl.ds(2 * ch, 2), 1], dr.at[b, pl.ds(2 * ch, 2)],
                     rx_s.at[n, ch], rx_r.at[n, ch], mate)

    def rs_u(n, b, j):
        return rcopy(ps.at[b, UP[(j + 1) // 2], 0, half(j % 2)], ru.at[b, j],
                     rs_s.at[n, 0, j], rs_r.at[n, 0, j], up)

    def rs_d(n, b, j):
        return rcopy(ps.at[b, DOWN[(j + 1) // 2], 0, half(1 - j % 2)], rd.at[b, j],
                     rs_s.at[n, 1, j], rs_r.at[n, 1, j], down)

    def rs_local(n, b, *chs):
        def f():
            for ch in chs:
                rs_l(n, b, ch).start()
        return f

    def rs_merge(n, b, *chs):
        def f():
            for ch in chs:
                rs_l(n, b, ch).wait_recv()
                for k in (2 * ch, 2 * ch + 1):
                    ps[b, k, 0] += dr[b, k]
        return f

    def rs_first(n, b):
        def f():
            rs_u(n, b, 0).start()
            rs_d(n, b, 0).start()
            rs_u(n, b, 1).start()
        return f

    def rs_second(n, b):
        def f():
            rs_d(n, b, 1).start()
        return f

    def rs_step(n, b, *js):
        def f():
            for j in js:
                k = (j + 3) // 2
                rs_u(n, b, j).wait_recv()
                ps[b, UP[k], 0, half(j % 2)] += ru[b, j]
                if j + 2 < 7:
                    rs_u(n, b, j + 2).start()
                rs_d(n, b, j).wait_recv()
                ps[b, DOWN[k], 0, half(1 - j % 2)] += rd[b, j]
                if j + 2 < 7:
                    rs_d(n, b, j + 2).start()
        return f

    def rs_sent(n, b):
        for j in range(7):
            rs_u(n, b, j).wait_send()
            rs_d(n, b, j).wait_send()
        for ch in range(4):
            rs_l(n, b, ch).wait_send()

    def token_loop(hooks, first, second):
        def at(it, p):
            for (i, q), fs in hooks.items():
                if q == p:
                    @pl.when(it == i)
                    def _():
                        for f in fs:
                            f()

        @pl.loop(0, 8)
        def _(it):
            e = it % 2
            ch = it // 2
            rows = pl.ds(pl.multiple_of(ch * R, R), R)
            at(it, 0)
            kept = first(ch, e, rows)
            if second is not None:
                at(it, 1)
                second(ch, e, rows, *kept)

    def gate(l, e, rows):
        return jnp.where(e == 0, gc_ref[rows, 2 * l:2 * l + 1], gc_ref[rows, 2 * l + 1:2 * l + 2])

    def rows_of(n, ch):
        return xg[n, pl.ds(2 * ch, 2)].reshape(R, -1)

    def put(b, ch, e, v):
        s = pl.ds(2 * ch, 2)
        ps[b, s] = jnp.where(e == 0, 0.0, ps[b, s]) + v.reshape(2, 2, T, v.shape[-1])

    def act(a1):
        sg = 1.0 / (1.0 + jnp.exp(-a1))
        return sg, a1 * sg

    def forward(l, n, b, ch, e, rows, a1s, a3s):
        g = gate(l, e, rows)
        u = rows_of(n, ch)
        a1 = _nn(u, w1[l, e])
        a3 = _nn(u, w3[l, e])
        sg, sl = act(a1)
        h = jnp.where(g >= 0, sl * a3, 0.0).astype(BF)
        a1s[...] = a1
        a3s[...] = a3
        hs[l, e, rows] = h
        put(b, ch, e, g * _nn(h, w2[l, e]).astype(BF).astype(F32))
        return ()

    def backward(l, nz, b, ch, e, rows, a1s, a3s):
        g = gate(l, e, rows)
        a1 = a1s[...]
        a3 = a3s[...]
        sg, sl = act(a1)
        h = hs[l, e, rows]
        r = _nt(rows_of(nz, ch), w2[l, e])
        dg = jnp.sum(h.astype(F32) * r, axis=1, keepdims=True)
        lane = lax.broadcasted_iota(jnp.int32, (R, 8), 1)
        dgc[rows, 0:8] = jnp.where(lane == 2 * l + e, dg, dgc[rows, 0:8])
        dh = g * r
        da3 = jnp.where(g >= 0, dh * sl, 0.0).astype(BF)
        da1 = jnp.where(g >= 0, dh * a3 * sg * (1.0 + a1 * (1.0 - sg)), 0.0).astype(BF)
        d1s[l, e, rows] = da1
        d3s[l, e, rows] = da3
        put(b, ch, e, (_nt(da1, w1[l, e]) + _nt(da3, w3[l, e])).astype(BF).astype(F32))
        return ()

    ag_start(0)
    gmsgs = []
    for k in range(8):
        q = (pos - REL[k] + 8) % 8
        for plane in range(2):
            if k == OWN and plane == 0:
                continue
            dev = _ring_ep(q, core + plane * (1 - 2 * core))
            c = rcopy(gts.at[pl.ds(dev * 8, 8)], gtr.at[pl.ds((k * 2 + plane) * 8, 8)],
                      g_s.at[k * 2 + plane], g_r.at[k * 2 + plane], dev)
            c.start()
            gmsgs.append(c)
    gtr[16 * OWN:16 * OWN + 8] = gts[pl.ds(pl.multiple_of(me * 8, 8), 8)]
    for c in wcopies[:3]:
        c.wait()
    for c in gmsgs:
        c.wait_recv()
    gct = gtr[...].T
    for b in range(16):
        gc_ref[b * T:(b + 1) * T, 0:8] = gct[0:T, b * 8:b * 8 + 8]

    token_loop({
        (0, 0): [ag_step(0, 0, 1), ag_have(0, 0, 1)],
        (1, 0): [ag_step(0, 2)],
        (2, 0): [ag_step(0, 3), ag_have(0, 2, 3), rs_local(0, 0, 0)],
        (3, 0): [ag_step(0, 4)],
        (4, 0): [ag_step(0, 5, 6), lambda: ag_start(1), ag_have(0, 4, 5), rs_local(0, 0, 1)],
        (6, 0): [rs_local(0, 0, 2), ag_have(0, 6, 7)],
        (7, 0): [rs_merge(0, 0, 2), rs_first(0, 0)],
    }, lambda ch, e, rows: forward(0, 0, 0, ch, e, rows, a1s.at[e, rows], a3s.at[e, rows]), None)
    rs_local(0, 0, 3)()
    rs_merge(0, 0, 0, 1, 3)()
    rs_second(0, 0)()
    for j in range(7):
        rs_step(0, 0, j)()
        ag_step(1, j)()
    xg[2, OWN, 0] = (x0_ref[...].astype(F32) + ps[0, OWN, 0]).astype(BF)
    ag_start(2)
    rs_sent(0, 0)
    for c in wcopies[3:]:
        c.wait()
    ag_have(1, *range(8))()

    token_loop({
        (0, 0): [ag_step(2, 0, 1), ag_have(2, 0, 1)],
        (0, 1): [ag_step(2, 2)],
        (1, 0): [ag_step(2, 3)],
        (1, 1): [ag_step(2, 4)],
        (2, 0): [ag_step(2, 5), ag_have(2, 2, 3), rs_local(2, 0, 0), rs_local(1, 1, 0)],
        (2, 1): [ag_step(2, 6)],
        (4, 0): [ag_have(2, 4, 5), rs_local(2, 0, 1), rs_local(1, 1, 1)],
        (6, 0): [rs_local(2, 0, 2), rs_local(1, 1, 2), ag_have(2, 6, 7)],
        (6, 1): [rs_merge(2, 0, 2), rs_first(2, 0), rs_merge(2, 0, 0, 1)],
        (7, 1): [rs_merge(1, 1, 2, 0, 1)],
    }, lambda ch, e, rows: forward(1, 2, 1, ch, e, rows, tmp1, tmp3),
        lambda ch, e, rows: backward(1, 1, 0, ch, e, rows, tmp1, tmp3))
    rs_local(2, 0, 3)()
    rs_local(1, 1, 3)()
    rs_merge(2, 0, 3)()
    rs_second(2, 0)()
    outs = []

    def out(src, dst, i):
        c = pltpu.make_async_copy(src, dst, osem.at[i])
        c.start()
        outs.append(c)
    for i, (s, d) in enumerate(((hs, h_o), (d1s, da1_o), (d3s, da3_o))):
        out(s.at[1], d.at[1], i)
    out(xg.at[0], xg_o.at[0], 3)
    out(xg.at[2], xg_o.at[1], 4)
    out(xg.at[1], zg_o.at[1], 5)
    rs_step(2, 0, *range(5))()
    rs_merge(1, 1, 3)()
    rs_step(2, 0, 5, 6)()
    xg[3, OWN, 0] = (dy_ref[...].astype(F32) + ps[0, OWN, 0]).astype(BF)
    ag_start(3)
    rs_sent(2, 0)

    token_loop({
        (0, 0): [ag_step(3, 0, 1), ag_have(3, 0, 1)],
        (1, 0): [ag_step(3, 2)],
        (2, 0): [ag_step(3, 3), ag_have(3, 2, 3), rs_local(3, 0, 0)],
        (3, 0): [ag_step(3, 4)],
        (4, 0): [ag_step(3, 5, 6), rs_first(1, 1), rs_second(1, 1), ag_have(3, 4, 5), rs_local(3, 0, 1)],
        (6, 0): [rs_local(3, 0, 2), ag_have(3, 6, 7)],
        (7, 0): [rs_merge(3, 0, 2), rs_first(3, 0), rs_step(1, 1, 0)],
    }, lambda ch, e, rows: backward(0, 3, 0, ch, e, rows, a1s.at[e, rows], a3s.at[e, rows]), None)
    rs_local(3, 0, 3)()
    rs_merge(3, 0, 0, 1, 3)()
    rs_second(3, 0)()
    out(xg.at[3], zg_o.at[0], 6)
    for i, (s, d) in enumerate(((hs, h_o), (d1s, da1_o), (d3s, da3_o))):
        out(s.at[0], d.at[0], 7 + i)

    dmsgs = []
    for k in range(8):
        t = dgc[k * 2 * T:(k + 1) * 2 * T].T[0:8]
        dgs[k * 16:k * 16 + 8] = t
        dgs[k * 16 + 8:k * 16 + 16] = pltpu.roll(t, T, 1)
        q = (pos + REL[k] + 8) % 8
        for plane in range(2):
            b = k * 2 + plane
            if k == OWN and plane == 0:
                continue
            dev = _ring_ep(q, core + plane * (1 - 2 * core))
            c = rcopy(dgs.at[pl.ds(b * 8, 8)], dgr_ref.at[pl.ds(me * 8, 8)], d_s.at[b], d_r.at[b], dev)
            c.start()
            dmsgs.append(c)
    dgr_ref[pl.ds(pl.multiple_of(me * 8, 8), 8)] = dgs[16 * OWN:16 * OWN + 8]

    for j in range(7):
        rs_step(3, 0, j)()
        if j < 6:
            rs_step(1, 1, j + 1)()
    dx0_ref[...] = (xg[3, OWN, 0].astype(F32) + ps[0, OWN, 0]).astype(BF)
    x2_ref[...] = (xg[2, OWN, 0].astype(F32) + ps[1, OWN, 0]).astype(BF)
    for c in dmsgs:
        c.wait_recv()
    for c in gmsgs + dmsgs:
        c.wait_send()
    for n in range(4):
        ag_sent(n)
    rs_sent(1, 1)
    rs_sent(3, 0)
    for c in outs:
        c.wait()


def _main(x0, dy, meta, ws):
    T, D = x0.shape
    EL, _, F = ws[0].shape
    N = 16 * T
    S = jax.ShapeDtypeStruct
    vm = pl.BlockSpec(memory_space=pltpu.VMEM)
    hb = pl.BlockSpec(memory_space=pl.ANY)
    dma = pltpu.SemaphoreType.DMA
    return pl.pallas_call(
        _main_kernel,
        out_shape=(S((T, D), BF), S((T, D), BF), S((128, 128), F32), S((N, 128), F32),
                   S((2, 8, 2, T, D), BF), S((2, 8, 2, T, D), BF),
                   S((2, EL, N, F), BF), S((2, EL, N, F), BF), S((2, EL, N, F), BF)),
        in_specs=[vm] * 3 + [hb] * 6,
        out_specs=(vm, vm, vm, vm) + (hb,) * 5,
        scratch_shapes=[
            pltpu.VMEM((2, EL, D, F), BF), pltpu.VMEM((2, EL, D, F), BF), pltpu.VMEM((2, EL, F, D), BF),
            pltpu.VMEM((4, 8, 2, T, D), BF),
            pltpu.VMEM((2, 8, 2, T, D), F32), pltpu.VMEM((2, 8, T, D), F32),
            pltpu.VMEM((2, 7, T // 2, D), F32), pltpu.VMEM((2, 7, T // 2, D), F32),
            pltpu.VMEM((EL, N, F), F32), pltpu.VMEM((EL, N, F), F32),
            pltpu.VMEM((2, EL, N, F), BF), pltpu.VMEM((2, EL, N, F), BF), pltpu.VMEM((2, EL, N, F), BF),
            pltpu.VMEM((128, 128), F32), pltpu.VMEM((128, 128), F32), pltpu.VMEM((N, 128), F32),
            pltpu.VMEM((128, 128), F32),
            pltpu.VMEM((4 * T, F), F32), pltpu.VMEM((4 * T, F), F32),
            dma((6,)), dma((4, 2, 7)), dma((4, 2, 7)), dma((4, 16)), dma((4, 16)),
            dma((4, 2, 7)), dma((4, 2, 7)), dma((4, 4)), dma((4, 4)),
            dma((16,)), dma((16,)), dma((16,)), dma((16,)), dma((10,)),
        ],
        compiler_params=pltpu.CompilerParams(collective_id=0, has_side_effects=True,
                                             vmem_limit_bytes=VMEM_LIMIT),
        name='moe',
    )(x0, dy, meta, *ws)


def _tn(a, b):
    return lax.dot_general(a, b, (((0,), (0,)), ((), ())), preferred_element_type=F32)


def _wgrad_kernel(x2_r, dx0_r, dgr, meta, gc, xg_h, zg_h, h_h, d1_h, d3_h,
                  x2_o, dx0_o, o1a, o3a, o2a, o1b, o3b, o2b, dga, dgb,
                  x, z, h, d1, d3, o1, o3, o2, isem, osem):
    T = x2_r.shape[0]
    ins = []
    for l in (1, 0):
        for i, (s, d) in enumerate(((xg_h, x), (d1_h, d1), (d3_h, d3), (zg_h, z), (h_h, h))):
            c = pltpu.make_async_copy(s.at[l], d.at[l], isem.at[l, i])
            c.start()
            ins.append(c)
    x2_o[...] = x2_r[...]
    dx0_o[...] = dx0_r[...]
    for l, o in ((0, dga), (1, dgb)):
        idx = meta[8 * l:8 * l + 8]
        acc = jnp.zeros((8, 128), F32)
        for i in range(16):
            for e in range(2):
                row = dgr[8 * i + 2 * l + e:8 * i + 2 * l + e + 1]
                acc = jnp.where(idx == float(2 * i + e), row, acc)
        o[...] = acc.T[0:T]
    outrefs = ((o1a, o3a, o2a), (o1b, o3b, o2b))

    def ocopy(l, i, e):
        return pltpu.make_async_copy((o1, o3, o2)[i].at[l, e], outrefs[l][i].at[e], osem.at[l, e, i])
    for n, l in enumerate((1, 0)):
        for c in ins[5 * n:5 * n + 5]:
            c.wait()

        @pl.loop(0, 2)
        def _(e):
            o1[l, e] = _tn(x[l], d1[l, e])
            ocopy(l, 0, e).start()
            o3[l, e] = _tn(x[l], d3[l, e])
            ocopy(l, 1, e).start()
            g = jnp.where(e == 0, gc[:, 2 * l:2 * l + 1], gc[:, 2 * l + 1:2 * l + 2])
            do = jnp.where(g >= 0, g * z[l].astype(F32), 0.0).astype(BF)
            o2[l, e] = _tn(h[l, e], do)
            ocopy(l, 2, e).start()
    for l in range(2):
        for e in range(2):
            for i in range(3):
                ocopy(l, i, e).wait()


def _wgrad(x2, dx0, dgr, meta, gc, xg, zg, h, d1, d3):
    T = x2.shape[0]
    _, N, D = xg.shape
    EL, F = h.shape[1], h.shape[3]
    S = jax.ShapeDtypeStruct
    vm = pl.BlockSpec(memory_space=pltpu.VMEM)
    hb = pl.BlockSpec(memory_space=pl.ANY)
    dma = pltpu.SemaphoreType.DMA
    up, dn = S((EL, D, F), F32), S((EL, F, D), F32)
    return pl.pallas_call(
        _wgrad_kernel,
        out_shape=(S((T, D), BF), S((T, D), BF), up, up, dn, up, up, dn, S((T, 8), F32), S((T, 8), F32)),
        in_specs=[vm] * 5 + [hb] * 5,
        out_specs=(vm, vm) + (hb,) * 6 + (vm, vm),
        scratch_shapes=[
            pltpu.VMEM((2, N, D), BF), pltpu.VMEM((2, N, D), BF), pltpu.VMEM((2, EL, N, F), BF),
            pltpu.VMEM((2, EL, N, F), BF), pltpu.VMEM((2, EL, N, F), BF),
            pltpu.VMEM((2, EL, D, F), F32), pltpu.VMEM((2, EL, D, F), F32), pltpu.VMEM((2, EL, F, D), F32),
            dma((2, 5)), dma((2, EL, 3)),
        ],
        compiler_params=pltpu.CompilerParams(vmem_limit_bytes=VMEM_LIMIT),
        name='wgrad',
    )(x2, dx0, dgr, meta, gc, xg, zg, h, d1, d3)


def solution(mesh):
    tok = P(('dp', 'ep'))
    wsp = P('ep')

    def body(x0, idx_a, g_a, idx_b, g_b, dy, *ws):
        T, D = x0.shape
        N = 16 * T
        meta = jnp.concatenate([idx_a.astype(F32), idx_b.astype(F32), g_a, g_b], axis=1).T
        meta = jnp.pad(meta, ((0, 0), (0, 128 - T)))
        x2, dx0, dgr, gc, xg, zg, h, d1, d3 = _main(x0, dy, meta, ws)
        return _wgrad(x2, dx0, dgr, meta, gc, xg.reshape(2, N, D), zg.reshape(2, N, D), h, d1, d3)

    return jax.shard_map(body, mesh=mesh,
                         in_specs=(tok,) * 6 + (wsp,) * 6,
                         out_specs=(tok,) * 10,
                         check_vma=False)
```

time: 528 us -> 200 us (0.38); the launches traced: 521 us -> 199 us
  waiting for transfers between devices: 315 us -> 0 us
  Pallas kernels: 0 us -> 193 us
  matrix products: 95.8 us -> 0 us
  blocking collectives: 44.5 us -> 0 us
  local copies, waits for them, and re-layouts: 30 us -> 3.45 us
  between operations: 14.9 us -> 0.66 us
  other arithmetic: 12.8 us -> 2.09 us
  starting transfers between devices: 8.03 us -> 0 us
    reduce_scatter x4 -> x0, waiting for transfers between devices: 206 us -> none  [the longest x2 114 us: _backward(): lax.psum_scatter(jnp.sum(du.astype(F32), axis=0), 'ep', scatter_dimension...]
    pallas_call x0 -> x2, Pallas kernels: none -> 193 us  [the longest x1 172 us: _main(): pl.pallas_call(_main_kernel, out_shape=(S((T, D), BF), S((T, D), BF), S((...]
    all_gather x4 -> x0, waiting for transfers between devices: 108 us -> none  [body(): ag = lambda v: lax.all_gather(v, 'ep', axis=0, tiled=True)]
    dot_general x18 -> x0, matrix products: 95.8 us -> none  [the longest x2 18.9 us: _backward(): r = jnp.einsum('rd,efd->erf', zb, w2, preferred_element_type=F32)]
    all_gather x2 -> x0, blocking collectives: 44.5 us -> none  [_gates(): gm = lax.all_gather(gm, 'ep', axis=0, tiled=True)]
    unnamed x78 -> x0, local copies, waits for them, and re-layouts: 29 us -> none
    convert_element_type x6 -> x2, other arithmetic: 9.44 us -> 1.38 us  [the longest x1 0.69 us: body(): idx_a.astype(F32)]
    all_to_all x2 -> x0, starting transfers between devices: 7.49 us -> none  [_backward(): dg = lax.all_to_all(dg.reshape(el, -1, t), 'ep', 1, 0, tiled=True)]
  transfers between devices with their start and end apart: 10 -> 0, of which waited for: 8 -> 0; matrix products, arithmetic and copies ran while one was open for 19% -> 0% of each run, Pallas kernels for 0% -> 0%
where the time goes in v2:
time: 200 us; the launch traced here: 199 us
  Pallas kernels  193 us (96%)
  local copies, waits for them, and re-layouts  3.45 us (2%)
  other arithmetic  2.09 us (1%)
    pallas_call x1, Pallas kernels, _main(): pl.pallas_call(_main_kernel, out_shape=(S((T, D), BF), S((T, D), BF), S((...  172 us
    pallas_call x1, Pallas kernels, _wgrad(): pl.pallas_call(_wgrad_kernel, out_shape=(S((T, D), BF), S((T, D), BF), up...  21.7 us

profile of v2, /device:TPU:0, one launch (start us, length us, event | category | flops | bytes accessed | tf_op | source)
XLA Modules:
  0.0 199.4 jit_solution(17395588738727393947)
XLA Ops:
  0.6 0.7 convert_element_type.8
  1.3 0.7 convert_element_type.9
  2.0 0.7 maximum_bitcast_fusion
  2.7 0.6 pad.4.meta_ref.meta
  3.3 171.5 %moe.1 = (bf16[64,1024]{1,0:T(8,128)(2,1)}, bf16[64,1024]{1,0:T(8,128)(2,1)}, f32[128,128]{1,0:T(8,128)}, f32[1024,128]{1,0:T(8,128)}, bf16[2,8,2,64,1024]{4,3,2...) custom-call(bf16[64,1024]{1,0:T(8,128)(2,1)} %x0_ref.1, ...), custom_call_target="tpu_custom_call" | custom-call | tf_op jit(solution)/shard_map/moe/pallas_call | solution.py:394
  174.9 21.7 %wgrad.1 = (bf16[64,1024]{1,0:T(8,128)(2,1)}, bf16[64,1024]{1,0:T(8,128)(2,1)}, f32[2,1024,512]{2,1,0:T(8,128)}, f32[2,1024,512]{2,1,0:T(8,128)}, f32[2,512,1024...) custom-call(bf16[64,1024]{1,0:T(8,128)(2,1)} %get-tuple-element.19.x, ...), custom_call_target="tpu_custom_call" | custom-call | tf_op jit(solution)/shard_map/wgrad/pallas_call | solution.py:478
  196.6 1.4 copy.22
  198.0 1.4 copy.23

commit v3 on v2

--- a/solution.py
+++ b/solution.py
@@ -10,10 +10,10 @@
 MESH = pl.DeviceIdType.MESH
 VMEM_LIMIT = 67043328
 
-REL = (-1, 0, -2, 1, 4, 3, -3, 2)
-OWN = 1
-UP = (4, 5, 7, 3, 1)
-DOWN = (4, 6, 2, 0, 1)
+REL = (-1, 1, -2, 2, -3, 3, 4, 0)
+OWN = 7
+UP = (6, 5, 3, 1, 7)
+DOWN = (6, 4, 2, 0, 7)
 
 
 def _ring_pos(ep):
@@ -35,7 +35,7 @@
     return jnp.dot(a, b, preferred_element_type=F32)
 
 
-def _main_kernel(x0_ref, dy_ref, meta_ref, w1a_h, w3a_h, w2a_h, w1b_h, w3b_h, w2b_h,
+def _main_kernel(x0_ref, dy_ref, ia_ref, ib_ref, ga_ref, gb_ref, w1a_h, w3a_h, w2a_h, w1b_h, w3b_h, w2b_h,
                  x2_ref, dx0_ref, dgr_ref, gc_ref, xg_o, zg_o, h_o, da1_o, da3_o,
                  w1, w3, w2, xg, ps, dr, ru, rd, a1s, a3s, hs, d1s, d3s, gts, gtr, dgc, dgs, tmp1, tmp3,
                  wsem, ag_s, ag_r, ax_s, ax_r, rs_s, rs_r, rx_s, rx_r, g_s, g_r, d_s, d_r, osem):
@@ -61,15 +61,13 @@
         pl.semaphore_signal(bar, inc=1, device_id={'ep': (me + i) % 16}, device_id_type=MESH)
     xg[0, OWN, 0] = x0_ref[...]
     xg[1, OWN, 0] = dy_ref[...]
-    for l in range(2):
-        idx = meta_ref[8 * l:8 * l + 8]
-        gate = meta_ref[16 + 8 * l:24 + 8 * l]
+    gts[...] = jnp.full_like(gts, -1.0)
+    for l, (ir, gr) in enumerate(((ia_ref, ga_ref), (ib_ref, gb_ref))):
+        idx, gt = ir[...], gr[...]
         for i in range(16):
             for e in range(2):
-                row = jnp.max(jnp.where(idx == float(2 * i + e), gate, -1.0), axis=0, keepdims=True)
-                gts[8 * i + 2 * l + e:8 * i + 2 * l + e + 1] = row
-    for i in range(16):
-        gts[8 * i + 4:8 * i + 8] = jnp.full((4, 128), -1.0, F32)
+                row = jnp.max(jnp.where(idx == 2 * i + e, gt, -1.0), axis=0, keepdims=True)
+                gts[8 * i + 2 * l + e:8 * i + 2 * l + e + 1, 0:T] = row
     dgc[...] = jnp.zeros_like(dgc)
     pl.semaphore_wait(bar, 15)
 
@@ -82,7 +80,7 @@
 
     pending = []
 
-    AU, AD = (1, 0, 2, 6, 4), (1, 3, 7, 5, 4)
+    AU, AD = (7, 0, 2, 4, 6), (7, 1, 3, 5, 6)
 
     def ag_u(n, j):
         i, h = j // 2, half(j % 2)
@@ -159,14 +157,14 @@
 
     def rs_first(n, b):
         def f():
+            rs_u(n, b, 1).start()
+            rs_d(n, b, 1).start()
+        return f
+
+    def rs_second(n, b):
+        def f():
             rs_u(n, b, 0).start()
             rs_d(n, b, 0).start()
-            rs_u(n, b, 1).start()
-        return f
-
-    def rs_second(n, b):
-        def f():
-            rs_d(n, b, 1).start()
         return f
 
     def rs_step(n, b, *js):
@@ -190,25 +188,26 @@
         for ch in range(4):
             rs_l(n, b, ch).wait_send()
 
-    def token_loop(hooks, first, second):
-        def at(it, p):
-            for (i, q), fs in hooks.items():
-                if q == p:
-                    @pl.when(it == i)
+    def token_loop(hooks, *stages):
+        ns = len(stages)
+
+        @pl.loop(0, 8 * ns)
+        def _(it):
+            for i, fs in hooks.items():
+                @pl.when(it == i)
+                def _():
+                    for f in fs:
+                        f()
+            ch = it // (2 * ns)
+            e = it % 2
+            rows = pl.ds(pl.multiple_of(ch * R, R), R)
+            if ns == 1:
+                stages[0](ch, e, rows)
+            else:
+                for k in range(ns):
+                    @pl.when((it // 2) % ns == k)
                     def _():
-                        for f in fs:
-                            f()
-
-        @pl.loop(0, 8)
-        def _(it):
-            e = it % 2
-            ch = it // 2
-            rows = pl.ds(pl.multiple_of(ch * R, R), R)
-            at(it, 0)
-            kept = first(ch, e, rows)
-            if second is not None:
-                at(it, 1)
-                second(ch, e, rows, *kept)
+                        stages[k](ch, e, rows)
 
     def gate(l, e, rows):
         return jnp.where(e == 0, gc_ref[rows, 2 * l:2 * l + 1], gc_ref[rows, 2 * l + 1:2 * l + 2])
@@ -277,77 +276,81 @@
         gc_ref[b * T:(b + 1) * T, 0:8] = gct[0:T, b * 8:b * 8 + 8]
 
     token_loop({
-        (0, 0): [ag_step(0, 0, 1), ag_have(0, 0, 1)],
-        (1, 0): [ag_step(0, 2)],
-        (2, 0): [ag_step(0, 3), ag_have(0, 2, 3), rs_local(0, 0, 0)],
-        (3, 0): [ag_step(0, 4)],
-        (4, 0): [ag_step(0, 5, 6), lambda: ag_start(1), ag_have(0, 4, 5), rs_local(0, 0, 1)],
-        (6, 0): [rs_local(0, 0, 2), ag_have(0, 6, 7)],
-        (7, 0): [rs_merge(0, 0, 2), rs_first(0, 0)],
-    }, lambda ch, e, rows: forward(0, 0, 0, ch, e, rows, a1s.at[e, rows], a3s.at[e, rows]), None)
+        0: [ag_step(0, 0, 1), ag_have(0, 0, 1)],
+        1: [ag_step(0, 2)],
+        2: [ag_step(0, 3), ag_have(0, 2, 3), rs_local(0, 0, 0)],
+        3: [ag_step(0, 4)],
+        4: [ag_step(0, 5), lambda: ag_start(1), ag_have(0, 4, 5)],
+        5: [ag_step(0, 6), rs_local(0, 0, 1)],
+        6: [rs_local(0, 0, 2), ag_have(0, 6, 7)],
+        7: [rs_merge(0, 0, 2), rs_first(0, 0), ag_step(1, 0, 1)],
+    }, lambda ch, e, rows: forward(0, 0, 0, ch, e, rows, a1s.at[e, rows], a3s.at[e, rows]))
     rs_local(0, 0, 3)()
     rs_merge(0, 0, 0, 1, 3)()
     rs_second(0, 0)()
-    for j in range(7):
-        rs_step(0, 0, j)()
-        ag_step(1, j)()
+    rs_step(0, 0, 1, 0, 3, 2, 5, 4)()
+    ag_step(1, 2, 3)()
+    rs_step(0, 0, 6)()
     xg[2, OWN, 0] = (x0_ref[...].astype(F32) + ps[0, OWN, 0]).astype(BF)
     ag_start(2)
     rs_sent(0, 0)
     for c in wcopies[3:]:
         c.wait()
-    ag_have(1, *range(8))()
 
     token_loop({
-        (0, 0): [ag_step(2, 0, 1), ag_have(2, 0, 1)],
-        (0, 1): [ag_step(2, 2)],
-        (1, 0): [ag_step(2, 3)],
-        (1, 1): [ag_step(2, 4)],
-        (2, 0): [ag_step(2, 5), ag_have(2, 2, 3), rs_local(2, 0, 0), rs_local(1, 1, 0)],
-        (2, 1): [ag_step(2, 6)],
-        (4, 0): [ag_have(2, 4, 5), rs_local(2, 0, 1), rs_local(1, 1, 1)],
-        (6, 0): [rs_local(2, 0, 2), rs_local(1, 1, 2), ag_have(2, 6, 7)],
-        (6, 1): [rs_merge(2, 0, 2), rs_first(2, 0), rs_merge(2, 0, 0, 1)],
-        (7, 1): [rs_merge(1, 1, 2, 0, 1)],
-    }, lambda ch, e, rows: forward(1, 2, 1, ch, e, rows, tmp1, tmp3),
-        lambda ch, e, rows: backward(1, 1, 0, ch, e, rows, tmp1, tmp3))
+        0: [ag_step(2, 0, 1), ag_have(2, 0, 1)],
+        1: [ag_step(2, 2), ag_step(1, 4)],
+        2: [ag_step(2, 3), ag_step(1, 5), ag_have(1, 0, 1)],
+        3: [ag_step(2, 4), ag_step(1, 6)],
+        4: [ag_step(2, 5), ag_have(2, 2, 3), rs_local(2, 0, 0), rs_local(1, 1, 0)],
+        5: [ag_step(2, 6)],
+        6: [ag_have(1, 2, 3)],
+        8: [ag_have(2, 4, 5), rs_local(2, 0, 1), rs_local(1, 1, 1)],
+        10: [rs_local(1, 1, 2), ag_have(1, 4, 5), rs_merge(1, 1, 0, 1)],
+        11: [rs_merge(1, 1, 2), rs_first(1, 1)],
+        12: [rs_local(2, 0, 2), ag_have(2, 6, 7)],
+        13: [rs_merge(2, 0, 2), rs_first(2, 0), rs_merge(2, 0, 0, 1)],
+        14: [rs_local(1, 1, 3), ag_have(1, 6, 7)],
+        15: [rs_merge(1, 1, 3), rs_second(1, 1)],
+    }, lambda ch, e, rows: forward(1, 2, 1, ch, e, rows, tmp1.at[e], tmp3.at[e]),
+        lambda ch, e, rows: backward(1, 1, 0, ch, e, rows, tmp1.at[e], tmp3.at[e]))
     rs_local(2, 0, 3)()
-    rs_local(1, 1, 3)()
-    rs_merge(2, 0, 3)()
-    rs_second(2, 0)()
     outs = []
 
     def out(src, dst, i):
         c = pltpu.make_async_copy(src, dst, osem.at[i])
         c.start()
         outs.append(c)
-    for i, (s, d) in enumerate(((hs, h_o), (d1s, da1_o), (d3s, da3_o))):
-        out(s.at[1], d.at[1], i)
+    for i, (sr, ds) in enumerate(((hs, h_o), (d1s, da1_o), (d3s, da3_o))):
+        out(sr.at[1], ds.at[1], i)
     out(xg.at[0], xg_o.at[0], 3)
     out(xg.at[2], xg_o.at[1], 4)
     out(xg.at[1], zg_o.at[1], 5)
-    rs_step(2, 0, *range(5))()
-    rs_merge(1, 1, 3)()
-    rs_step(2, 0, 5, 6)()
+    rs_merge(2, 0, 3)()
+    rs_second(2, 0)()
+    rs_step(2, 0, 1, 0, 3, 2, 5, 4)()
+    rs_step(1, 1, 1)()
+    rs_step(2, 0, 6)()
     xg[3, OWN, 0] = (dy_ref[...].astype(F32) + ps[0, OWN, 0]).astype(BF)
     ag_start(3)
     rs_sent(2, 0)
 
     token_loop({
-        (0, 0): [ag_step(3, 0, 1), ag_have(3, 0, 1)],
-        (1, 0): [ag_step(3, 2)],
-        (2, 0): [ag_step(3, 3), ag_have(3, 2, 3), rs_local(3, 0, 0)],
-        (3, 0): [ag_step(3, 4)],
-        (4, 0): [ag_step(3, 5, 6), rs_first(1, 1), rs_second(1, 1), ag_have(3, 4, 5), rs_local(3, 0, 1)],
-        (6, 0): [rs_local(3, 0, 2), ag_have(3, 6, 7)],
-        (7, 0): [rs_merge(3, 0, 2), rs_first(3, 0), rs_step(1, 1, 0)],
-    }, lambda ch, e, rows: backward(0, 3, 0, ch, e, rows, a1s.at[e, rows], a3s.at[e, rows]), None)
+        0: [ag_step(3, 0, 1), ag_have(3, 0, 1)],
+        1: [ag_step(3, 2)],
+        2: [ag_step(3, 3), ag_have(3, 2, 3), rs_local(3, 0, 0)],
+        3: [ag_step(3, 4)],
+        4: [ag_step(3, 5), rs_step(1, 1, 0), ag_have(3, 4, 5)],
+        5: [ag_step(3, 6), rs_step(1, 1, 3), rs_local(3, 0, 1)],
+        6: [rs_local(3, 0, 2), ag_have(3, 6, 7)],
+        7: [rs_merge(3, 0, 2), rs_first(3, 0)],
+    }, lambda ch, e, rows: backward(0, 3, 0, ch, e, rows, a1s.at[e, rows], a3s.at[e, rows]))
     rs_local(3, 0, 3)()
+    out(xg.at[3], zg_o.at[0], 6)
+    for i, (sr, ds) in enumerate(((hs, h_o), (d1s, da1_o), (d3s, da3_o))):
+        out(sr.at[0], ds.at[0], 7 + i)
     rs_merge(3, 0, 0, 1, 3)()
     rs_second(3, 0)()
-    out(xg.at[3], zg_o.at[0], 6)
-    for i, (s, d) in enumerate(((hs, h_o), (d1s, da1_o), (d3s, da3_o))):
-        out(s.at[0], d.at[0], 7 + i)
 
     dmsgs = []
     for k in range(8):
@@ -365,10 +368,13 @@
             dmsgs.append(c)
     dgr_ref[pl.ds(pl.multiple_of(me * 8, 8), 8)] = dgs[16 * OWN:16 * OWN + 8]
 
-    for j in range(7):
-        rs_step(3, 0, j)()
-        if j < 6:
-            rs_step(1, 1, j + 1)()
+    rs_step(3, 0, 1, 0)()
+    rs_step(1, 1, 2)()
+    rs_step(3, 0, 3, 2)()
+    rs_step(1, 1, 5, 4)()
+    rs_step(3, 0, 5, 4)()
+    rs_step(1, 1, 6)()
+    rs_step(3, 0, 6)()
     dx0_ref[...] = (xg[3, OWN, 0].astype(F32) + ps[0, OWN, 0]).astype(BF)
     x2_ref[...] = (xg[2, OWN, 0].astype(F32) + ps[1, OWN, 0]).astype(BF)
     for c in dmsgs:
@@ -396,7 +402,7 @@
         out_shape=(S((T, D), BF), S((T, D), BF), S((128, 128), F32), S((N, 128), F32),
                    S((2, 8, 2, T, D), BF), S((2, 8, 2, T, D), BF),
                    S((2, EL, N, F), BF), S((2, EL, N, F), BF), S((2, EL, N, F), BF)),
-        in_specs=[vm] * 3 + [hb] * 6,
+        in_specs=[vm] * 6 + [hb] * 6,
         out_specs=(vm, vm, vm, vm) + (hb,) * 5,
         scratch_shapes=[
             pltpu.VMEM((2, EL, D, F), BF), pltpu.VMEM((2, EL, D, F), BF), pltpu.VMEM((2, EL, F, D), BF),
@@ -407,7 +413,7 @@
             pltpu.VMEM((2, EL, N, F), BF), pltpu.VMEM((2, EL, N, F), BF), pltpu.VMEM((2, EL, N, F), BF),
             pltpu.VMEM((128, 128), F32), pltpu.VMEM((128, 128), F32), pltpu.VMEM((N, 128), F32),
             pltpu.VMEM((128, 128), F32),
-            pltpu.VMEM((4 * T, F), F32), pltpu.VMEM((4 * T, F), F32),
+            pltpu.VMEM((EL, 4 * T, F), F32), pltpu.VMEM((EL, 4 * T, F), F32),
             dma((6,)), dma((4, 2, 7)), dma((4, 2, 7)), dma((4, 16)), dma((4, 16)),
             dma((4, 2, 7)), dma((4, 2, 7)), dma((4, 4)), dma((4, 4)),
             dma((16,)), dma((16,)), dma((16,)), dma((16,)), dma((10,)),
@@ -415,14 +421,14 @@
         compiler_params=pltpu.CompilerParams(collective_id=0, has_side_effects=True,
                                              vmem_limit_bytes=VMEM_LIMIT),
         name='moe',
-    )(x0, dy, meta, *ws)
+    )(x0, dy, *meta, *ws)
 
 
 def _tn(a, b):
     return lax.dot_general(a, b, (((0,), (0,)), ((), ())), preferred_element_type=F32)
 
 
-def _wgrad_kernel(x2_r, dx0_r, dgr, meta, gc, xg_h, zg_h, h_h, d1_h, d3_h,
+def _wgrad_kernel(x2_r, dx0_r, dgr, ia_ref, ib_ref, gc, xg_h, zg_h, h_h, d1_h, d3_h,
                   x2_o, dx0_o, o1a, o3a, o2a, o1b, o3b, o2b, dga, dgb,
                   x, z, h, d1, d3, o1, o3, o2, isem, osem):
     T = x2_r.shape[0]
@@ -434,20 +440,20 @@
             ins.append(c)
     x2_o[...] = x2_r[...]
     dx0_o[...] = dx0_r[...]
-    for l, o in ((0, dga), (1, dgb)):
-        idx = meta[8 * l:8 * l + 8]
-        acc = jnp.zeros((8, 128), F32)
+    for l, ir, o in ((0, ia_ref, dga), (1, ib_ref, dgb)):
+        idx = ir[...]
+        acc = jnp.zeros((8, T), F32)
         for i in range(16):
             for e in range(2):
-                row = dgr[8 * i + 2 * l + e:8 * i + 2 * l + e + 1]
-                acc = jnp.where(idx == float(2 * i + e), row, acc)
-        o[...] = acc.T[0:T]
+                row = dgr[8 * i + 2 * l + e:8 * i + 2 * l + e + 1, 0:T]
+                acc = jnp.where(idx == 2 * i + e, row, acc)
+        o[...] = acc
     outrefs = ((o1a, o3a, o2a), (o1b, o3b, o2b))
 
     def ocopy(l, i, e):
         return pltpu.make_async_copy((o1, o3, o2)[i].at[l, e], outrefs[l][i].at[e], osem.at[l, e, i])
     for n, l in enumerate((1, 0)):
-        for c in ins[5 * n:5 * n + 5]:
+        for c in ins[5 * n:5 * n + 3]:
             c.wait()
 
         @pl.loop(0, 2)
@@ -456,6 +462,11 @@
             ocopy(l, 0, e).start()
             o3[l, e] = _tn(x[l], d3[l, e])
             ocopy(l, 1, e).start()
+        for c in ins[5 * n + 3:5 * n + 5]:
+            c.wait()
+
+        @pl.loop(0, 2)
+        def _(e):
             g = jnp.where(e == 0, gc[:, 2 * l:2 * l + 1], gc[:, 2 * l + 1:2 * l + 2])
             do = jnp.where(g >= 0, g * z[l].astype(F32), 0.0).astype(BF)
             o2[l, e] = _tn(h[l, e], do)
@@ -477,8 +488,8 @@
     up, dn = S((EL, D, F), F32), S((EL, F, D), F32)
     return pl.pallas_call(
         _wgrad_kernel,
-        out_shape=(S((T, D), BF), S((T, D), BF), up, up, dn, up, up, dn, S((T, 8), F32), S((T, 8), F32)),
-        in_specs=[vm] * 5 + [hb] * 5,
+        out_shape=(S((T, D), BF), S((T, D), BF), up, up, dn, up, up, dn, S((8, T), F32), S((8, T), F32)),
+        in_specs=[vm] * 6 + [hb] * 5,
         out_specs=(vm, vm) + (hb,) * 6 + (vm, vm),
         scratch_shapes=[
             pltpu.VMEM((2, N, D), BF), pltpu.VMEM((2, N, D), BF), pltpu.VMEM((2, EL, N, F), BF),
@@ -488,7 +499,7 @@
         ],
         compiler_params=pltpu.CompilerParams(vmem_limit_bytes=VMEM_LIMIT),
         name='wgrad',
-    )(x2, dx0, dgr, meta, gc, xg, zg, h, d1, d3)
+    )(x2, dx0, dgr, *meta, gc, xg, zg, h, d1, d3)
 
 
 def solution(mesh):
@@ -498,10 +509,10 @@
     def body(x0, idx_a, g_a, idx_b, g_b, dy, *ws):
         T, D = x0.shape
         N = 16 * T
-        meta = jnp.concatenate([idx_a.astype(F32), idx_b.astype(F32), g_a, g_b], axis=1).T
-        meta = jnp.pad(meta, ((0, 0), (0, 128 - T)))
-        x2, dx0, dgr, gc, xg, zg, h, d1, d3 = _main(x0, dy, meta, ws)
-        return _wgrad(x2, dx0, dgr, meta, gc, xg.reshape(2, N, D), zg.reshape(2, N, D), h, d1, d3)
+        ids = (idx_a.T, idx_b.T)
+        x2, dx0, dgr, gc, xg, zg, h, d1, d3 = _main(x0, dy, ids + (g_a.T, g_b.T), ws)
+        r = _wgrad(x2, dx0, dgr, ids, gc, xg.reshape(2, N, D), zg.reshape(2, N, D), h, d1, d3)
+        return tuple(r[:8]) + (r[8].T, r[9].T)
 
     return jax.shard_map(body, mesh=mesh,
                          in_specs=(tok,) * 6 + (wsp,) * 6,

time: 200 us -> 190 us (0.950)
  Pallas kernels: 193 us -> 189 us
  local copies, waits for them, and re-layouts: 3.45 us -> 0 us
  other arithmetic: 2.09 us -> 0 us
    pallas_call x1, Pallas kernels: 172 us -> 166 us  [_main(): pl.pallas_call(_main_kernel, out_shape=(S((T, D), BF), S((T, D), BF), S((...]
    pallas_call x2 -> x0, local copies, waits for them, and re-layouts: 2.84 us -> none  [_wgrad(): pl.pallas_call(_wgrad_kernel, out_shape=(S((T, D), BF), S((T, D), BF), up...]
where the time goes in v3:
time: 190 us
  Pallas kernels  189 us (99%)
    pallas_call x1, Pallas kernels, _main(): pl.pallas_call(_main_kernel, out_shape=(S((T, D), BF), S((T, D), BF), S((...  166 us
    pallas_call x1, Pallas kernels, _wgrad(): pl.pallas_call(_wgrad_kernel, out_shape=(S((T, D), BF), S((T, D), BF), up...  22.8 us

profile of v3, /device:TPU:0, one launch (start us, length us, event | category | flops | bytes accessed | tf_op | source)
XLA Modules:
  0.0 189.8 jit_solution(14637169856810390044)
XLA Ops:
  0.6 166.1 %moe.1 = (bf16[64,1024]{1,0:T(8,128)(2,1)}, bf16[64,1024]{1,0:T(8,128)(2,1)}, f32[128,128]{1,0:T(8,128)}, f32[1024,128]{1,0:T(8,128)}, bf16[2,8,2,64,1024]{4,3,2...) custom-call(bf16[64,1024]{1,0:T(8,128)(2,1)} %x0_ref.1, ...), custom_call_target="tpu_custom_call" | custom-call | tf_op jit(solution)/shard_map/moe/pallas_call | solution.py:400
  166.8 22.8 %wgrad.1 = (bf16[64,1024]{1,0:T(8,128)(2,1)}, bf16[64,1024]{1,0:T(8,128)(2,1)}, f32[2,1024,512]{2,1,0:T(8,128)}, f32[2,1024,512]{2,1,0:T(8,128)}, f32[2,512,1024...) custom-call(bf16[64,1024]{1,0:T(8,128)(2,1)} %get-tuple-element.29.x, ...), custom_call_target="tpu_custom_call" | custom-call | tf_op jit(solution)/shard_map/wgrad/pallas_call | solution.py:489

commit v4 on v3

--- a/solution.py
+++ b/solution.py
@@ -37,11 +37,15 @@
 
 def _main_kernel(x0_ref, dy_ref, ia_ref, ib_ref, ga_ref, gb_ref, w1a_h, w3a_h, w2a_h, w1b_h, w3b_h, w2b_h,
                  x2_ref, dx0_ref, dgr_ref, gc_ref, xg_o, zg_o, h_o, da1_o, da3_o,
-                 w1, w3, w2, xg, ps, dr, ru, rd, a1s, a3s, hs, d1s, d3s, gts, gtr, dgc, dgs, tmp1, tmp3,
-                 wsem, ag_s, ag_r, ax_s, ax_r, rs_s, rs_r, rx_s, rx_r, g_s, g_r, d_s, d_r, osem):
+                 w1, w3, w2, xg, ps, dr, ru, rd, a1s, a3s, hs, d1s, d3s, gq, gtr, dgc, dgs, tmp1, tmp3,
+                 wsem, gq_s, gq_r, gx_s, gx_r, ag_s, ag_r, ax_s, ax_r, rs_s, rs_r, rx_s, rx_r, d_s, d_r, osem):
     T = x0_ref.shape[0]
     H = T // 2
     R = 4 * T
+    xin = [pltpu.make_async_copy(r, xg.at[n, OWN, 0], osem.at[n])
+           for n, r in enumerate((x0_ref, dy_ref))]
+    for c in xin:
+        c.start()
     me = lax.axis_index('ep')
     core = me % 2
     pos = _ring_pos(me)
@@ -57,59 +61,102 @@
             wcopies.append(c)
 
     bar = pltpu.get_barrier_semaphore()
-    for i in range(1, 16):
-        pl.semaphore_signal(bar, inc=1, device_id={'ep': (me + i) % 16}, device_id_type=MESH)
-    xg[0, OWN, 0] = x0_ref[...]
-    xg[1, OWN, 0] = dy_ref[...]
-    gts[...] = jnp.full_like(gts, -1.0)
+    for dev in (up, down, mate):
+        pl.semaphore_signal(bar, inc=1, device_id={'ep': dev}, device_id_type=MESH)
     for l, (ir, gr) in enumerate(((ia_ref, ga_ref), (ib_ref, gb_ref))):
-        idx, gt = ir[...], gr[...]
-        for i in range(16):
-            for e in range(2):
-                row = jnp.max(jnp.where(idx == 2 * i + e, gt, -1.0), axis=0, keepdims=True)
-                gts[8 * i + 2 * l + e:8 * i + 2 * l + e + 1, 0:T] = row
+        gq[OWN, 0, 8 * l:8 * l + 8, 0:T] = ir[...].astype(F32)
+        gq[OWN, 0, 8 * l:8 * l + 8, T:2 * T] = gr[...]
+    gtr[...] = jnp.full_like(gtr, -1.0)
     dgc[...] = jnp.zeros_like(dgc)
-    pl.semaphore_wait(bar, 15)
+    for c in xin:
+        c.wait()
+    pl.semaphore_wait(bar, 3)
 
     def rcopy(src, dst, ss, rs, dev):
         return pltpu.make_async_remote_copy(src_ref=src, dst_ref=dst, send_sem=ss, recv_sem=rs,
                                             device_id={'ep': dev}, device_id_type=MESH)
 
+    Q = H // 2
+
     def half(i):
         return pl.ds(i * H, H)
 
+    def quarter(i, q):
+        return pl.ds(i * H + q * Q, Q)
+
     pending = []
 
     AU, AD = (7, 0, 2, 4, 6), (7, 1, 3, 5, 6)
 
-    def ag_u(n, j):
-        i, h = j // 2, half(j % 2)
-        return rcopy(xg.at[n, AU[i], 0, h], xg.at[n, AU[i + 1], 0, h], ag_s.at[n, 0, j], ag_r.at[n, 0, j], up)
-
-    def ag_d(n, j):
-        i, h = j // 2, half(1 - j % 2)
-        return rcopy(xg.at[n, AD[i], 0, h], xg.at[n, AD[i + 1], 0, h], ag_s.at[n, 1, j], ag_r.at[n, 1, j], down)
+    def ag_u(n, j, q):
+        i, h, m = j // 2, quarter(j % 2, q), 2 * j + q
+        return rcopy(xg.at[n, AU[i], 0, h], xg.at[n, AU[i + 1], 0, h], ag_s.at[n, 0, m], ag_r.at[n, 0, m], up)
+
+    def ag_d(n, j, q):
+        i, h, m = j // 2, quarter(1 - j % 2, q), 2 * j + q
+        return rcopy(xg.at[n, AD[i], 0, h], xg.at[n, AD[i + 1], 0, h], ag_s.at[n, 1, m], ag_r.at[n, 1, m], down)
 
     def ag_m(n, k, hf):
         return rcopy(xg.at[n, k, 0, half(hf)], xg.at[n, k, 1, half(hf)],
                      ax_s.at[n, k * 2 + hf], ax_r.at[n, k * 2 + hf], mate)
 
+    def gq_u(h):
+        return rcopy(gq.at[AU[h], 0], gq.at[AU[h + 1], 0], gq_s.at[0, h], gq_r.at[0, h], up)
+
+    def gq_d(h):
+        return rcopy(gq.at[AD[h], 0], gq.at[AD[h + 1], 0], gq_s.at[1, h], gq_r.at[1, h], down)
+
+    def gq_m(k):
+        return rcopy(gq.at[k, 0], gq.at[k, 1], gx_s.at[k], gx_r.at[k], mate)
+
+    def gq_step(h):
+        def f():
+            gq_u(h).wait_recv()
+            if h < 3:
+                gq_u(h + 1).start()
+            gq_m(AU[h + 1]).start()
+            if h < 3:
+                gq_d(h).wait_recv()
+                if h < 2:
+                    gq_d(h + 1).start()
+                gq_m(AD[h + 1]).start()
+        return f
+
+    def gates(ch):
+        def f():
+            for k in (2 * ch, 2 * ch + 1):
+                gq_m(k).wait_recv()
+                for plane in range(2):
+                    for l in range(2):
+                        t = gq[k, plane, 8 * l:8 * l + 8]
+                        gt = pltpu.roll(t, T, 1)
+                        for e in range(2):
+                            row = 8 * (2 * k + plane) + 2 * l + e
+                            mine = (2 * me + e).astype(F32)
+                            gtr[row:row + 1] = jnp.max(jnp.where(t == mine, gt, -1.0), axis=0, keepdims=True)
+            gct = gtr[...].T
+            for b in range(4 * ch, 4 * ch + 4):
+                gc_ref[b * T:(b + 1) * T, 0:8] = gct[0:T, b * 8:b * 8 + 8]
+        return f
+
     def ag_start(n):
         for j in range(2):
-            ag_u(n, j).start()
-            ag_d(n, j).start()
+            for q in range(2):
+                ag_u(n, j, q).start()
+                ag_d(n, j, q).start()
         for hf in range(2):
             ag_m(n, OWN, hf).start()
 
     def ag_step(n, *js):
         def f():
             for j in js:
-                ag_u(n, j).wait_recv()
-                if j + 2 < 7:
-                    ag_u(n, j + 2).start()
-                ag_d(n, j).wait_recv()
-                if j + 2 < 7:
-                    ag_d(n, j + 2).start()
+                for q in range(2):
+                    ag_u(n, j, q).wait_recv()
+                    if j + 2 < 7:
+                        ag_u(n, j + 2, q).start()
+                    ag_d(n, j, q).wait_recv()
+                    if j + 2 < 7:
+                        ag_d(n, j + 2, q).start()
                 ag_m(n, AU[j // 2 + 1], j % 2).start()
                 ag_m(n, AD[j // 2 + 1], 1 - j % 2).start()
         return f
@@ -123,8 +170,9 @@
 
     def ag_sent(n):
         for j in range(7):
-            ag_u(n, j).wait_send()
-            ag_d(n, j).wait_send()
+            for q in range(2):
+                ag_u(n, j, q).wait_send()
+                ag_d(n, j, q).wait_send()
         for k in range(8):
             for hf in range(2):
                 ag_m(n, k, hf).wait_send()
@@ -133,13 +181,15 @@
         return rcopy(ps.at[b, pl.ds(2 * ch, 2), 1], dr.at[b, pl.ds(2 * ch, 2)],
                      rx_s.at[n, ch], rx_r.at[n, ch], mate)
 
-    def rs_u(n, b, j):
-        return rcopy(ps.at[b, UP[(j + 1) // 2], 0, half(j % 2)], ru.at[b, j],
-                     rs_s.at[n, 0, j], rs_r.at[n, 0, j], up)
-
-    def rs_d(n, b, j):
-        return rcopy(ps.at[b, DOWN[(j + 1) // 2], 0, half(1 - j % 2)], rd.at[b, j],
-                     rs_s.at[n, 1, j], rs_r.at[n, 1, j], down)
+    def rs_u(n, b, j, q):
+        m = 2 * j + q
+        return rcopy(ps.at[b, UP[(j + 1) // 2], 0, quarter(j % 2, q)], ru.at[b, j, quarter(0, q)],
+                     rs_s.at[n, 0, m], rs_r.at[n, 0, m], up)
+
+    def rs_d(n, b, j, q):
+        m = 2 * j + q
+        return rcopy(ps.at[b, DOWN[(j + 1) // 2], 0, quarter(1 - j % 2, q)], rd.at[b, j, quarter(0, q)],
+                     rs_s.at[n, 1, m], rs_r.at[n, 1, m], down)
 
     def rs_local(n, b, *chs):
         def f():
@@ -157,34 +207,38 @@
 
     def rs_first(n, b):
         def f():
-            rs_u(n, b, 1).start()
-            rs_d(n, b, 1).start()
+            for q in range(2):
+                rs_u(n, b, 1, q).start()
+                rs_d(n, b, 1, q).start()
         return f
 
     def rs_second(n, b):
         def f():
-            rs_u(n, b, 0).start()
-            rs_d(n, b, 0).start()
+            for q in range(2):
+                rs_u(n, b, 0, q).start()
+                rs_d(n, b, 0, q).start()
         return f
 
     def rs_step(n, b, *js):
         def f():
             for j in js:
                 k = (j + 3) // 2
-                rs_u(n, b, j).wait_recv()
-                ps[b, UP[k], 0, half(j % 2)] += ru[b, j]
-                if j + 2 < 7:
-                    rs_u(n, b, j + 2).start()
-                rs_d(n, b, j).wait_recv()
-                ps[b, DOWN[k], 0, half(1 - j % 2)] += rd[b, j]
-                if j + 2 < 7:
-                    rs_d(n, b, j + 2).start()
+                for q in range(2):
+                    rs_u(n, b, j, q).wait_recv()
+                    ps[b, UP[k], 0, quarter(j % 2, q)] += ru[b, j, quarter(0, q)]
+                    if j + 2 < 7:
+                        rs_u(n, b, j + 2, q).start()
+                    rs_d(n, b, j, q).wait_recv()
+                    ps[b, DOWN[k], 0, quarter(1 - j % 2, q)] += rd[b, j, quarter(0, q)]
+                    if j + 2 < 7:
+                        rs_d(n, b, j + 2, q).start()
         return f
 
     def rs_sent(n, b):
         for j in range(7):
-            rs_u(n, b, j).wait_send()
-            rs_d(n, b, j).wait_send()
+            for q in range(2):
+                rs_u(n, b, j, q).wait_send()
+                rs_d(n, b, j, q).wait_send()
         for ch in range(4):
             rs_l(n, b, ch).wait_send()
 
@@ -254,35 +308,20 @@
         put(b, ch, e, (_nt(da1, w1[l, e]) + _nt(da3, w3[l, e])).astype(BF).astype(F32))
         return ()
 
+    gq_u(0).start()
+    gq_d(0).start()
+    gq_m(OWN).start()
     ag_start(0)
-    gmsgs = []
-    for k in range(8):
-        q = (pos - REL[k] + 8) % 8
-        for plane in range(2):
-            if k == OWN and plane == 0:
-                continue
-            dev = _ring_ep(q, core + plane * (1 - 2 * core))
-            c = rcopy(gts.at[pl.ds(dev * 8, 8)], gtr.at[pl.ds((k * 2 + plane) * 8, 8)],
-                      g_s.at[k * 2 + plane], g_r.at[k * 2 + plane], dev)
-            c.start()
-            gmsgs.append(c)
-    gtr[16 * OWN:16 * OWN + 8] = gts[pl.ds(pl.multiple_of(me * 8, 8), 8)]
     for c in wcopies[:3]:
         c.wait()
-    for c in gmsgs:
-        c.wait_recv()
-    gct = gtr[...].T
-    for b in range(16):
-        gc_ref[b * T:(b + 1) * T, 0:8] = gct[0:T, b * 8:b * 8 + 8]
-
     token_loop({
-        0: [ag_step(0, 0, 1), ag_have(0, 0, 1)],
-        1: [ag_step(0, 2)],
-        2: [ag_step(0, 3), ag_have(0, 2, 3), rs_local(0, 0, 0)],
-        3: [ag_step(0, 4)],
-        4: [ag_step(0, 5), lambda: ag_start(1), ag_have(0, 4, 5)],
-        5: [ag_step(0, 6), rs_local(0, 0, 1)],
-        6: [rs_local(0, 0, 2), ag_have(0, 6, 7)],
+        0: [gq_step(0), ag_step(0, 0, 1), gates(0), ag_have(0, 0, 1)],
+        1: [gq_step(1), ag_step(0, 2)],
+        2: [ag_step(0, 3), gates(1), ag_have(0, 2, 3), rs_local(0, 0, 0)],
+        3: [gq_step(2), ag_step(0, 4)],
+        4: [ag_step(0, 5), lambda: ag_start(1), gates(2), ag_have(0, 4, 5)],
+        5: [gq_step(3), ag_step(0, 6), rs_local(0, 0, 1)],
+        6: [rs_local(0, 0, 2), gates(3), ag_have(0, 6, 7)],
         7: [rs_merge(0, 0, 2), rs_first(0, 0), ag_step(1, 0, 1)],
     }, lambda ch, e, rows: forward(0, 0, 0, ch, e, rows, a1s.at[e, rows], a3s.at[e, rows]))
     rs_local(0, 0, 3)()
@@ -291,7 +330,7 @@
     rs_step(0, 0, 1, 0, 3, 2, 5, 4)()
     ag_step(1, 2, 3)()
     rs_step(0, 0, 6)()
-    xg[2, OWN, 0] = (x0_ref[...].astype(F32) + ps[0, OWN, 0]).astype(BF)
+    xg[2, OWN, 0] = (xg[0, OWN, 0].astype(F32) + ps[0, OWN, 0]).astype(BF)
     ag_start(2)
     rs_sent(0, 0)
     for c in wcopies[3:]:
@@ -331,7 +370,7 @@
     rs_step(2, 0, 1, 0, 3, 2, 5, 4)()
     rs_step(1, 1, 1)()
     rs_step(2, 0, 6)()
-    xg[3, OWN, 0] = (dy_ref[...].astype(F32) + ps[0, OWN, 0]).astype(BF)
+    xg[3, OWN, 0] = (xg[1, OWN, 0].astype(F32) + ps[0, OWN, 0]).astype(BF)
     ag_start(3)
     rs_sent(2, 0)
 
@@ -379,7 +418,7 @@
     x2_ref[...] = (xg[2, OWN, 0].astype(F32) + ps[1, OWN, 0]).astype(BF)
     for c in dmsgs:
         c.wait_recv()
-    for c in gmsgs + dmsgs:
+    for c in dmsgs + [gq_u(h) for h in range(4)] + [gq_d(h) for h in range(3)] + [gq_m(k) for k in range(8)]:
         c.wait_send()
     for n in range(4):
         ag_sent(n)
@@ -402,7 +441,7 @@
         out_shape=(S((T, D), BF), S((T, D), BF), S((128, 128), F32), S((N, 128), F32),
                    S((2, 8, 2, T, D), BF), S((2, 8, 2, T, D), BF),
                    S((2, EL, N, F), BF), S((2, EL, N, F), BF), S((2, EL, N, F), BF)),
-        in_specs=[vm] * 6 + [hb] * 6,
+        in_specs=[hb] * 2 + [vm] * 4 + [hb] * 6,
         out_specs=(vm, vm, vm, vm) + (hb,) * 5,
         scratch_shapes=[
             pltpu.VMEM((2, EL, D, F), BF), pltpu.VMEM((2, EL, D, F), BF), pltpu.VMEM((2, EL, F, D), BF),
@@ -411,12 +450,13 @@
             pltpu.VMEM((2, 7, T // 2, D), F32), pltpu.VMEM((2, 7, T // 2, D), F32),
             pltpu.VMEM((EL, N, F), F32), pltpu.VMEM((EL, N, F), F32),
             pltpu.VMEM((2, EL, N, F), BF), pltpu.VMEM((2, EL, N, F), BF), pltpu.VMEM((2, EL, N, F), BF),
-            pltpu.VMEM((128, 128), F32), pltpu.VMEM((128, 128), F32), pltpu.VMEM((N, 128), F32),
+            pltpu.VMEM((8, 2, 16, 128), F32), pltpu.VMEM((128, 128), F32), pltpu.VMEM((N, 128), F32),
             pltpu.VMEM((128, 128), F32),
             pltpu.VMEM((EL, 4 * T, F), F32), pltpu.VMEM((EL, 4 * T, F), F32),
-            dma((6,)), dma((4, 2, 7)), dma((4, 2, 7)), dma((4, 16)), dma((4, 16)),
-            dma((4, 2, 7)), dma((4, 2, 7)), dma((4, 4)), dma((4, 4)),
-            dma((16,)), dma((16,)), dma((16,)), dma((16,)), dma((10,)),
+            dma((6,)), dma((2, 4)), dma((2, 4)), dma((8,)), dma((8,)),
+            dma((4, 2, 14)), dma((4, 2, 14)), dma((4, 16)), dma((4, 16)),
+            dma((4, 2, 14)), dma((4, 2, 14)), dma((4, 4)), dma((4, 4)),
+            dma((16,)), dma((16,)), dma((10,)),
         ],
         compiler_params=pltpu.CompilerParams(collective_id=0, has_side_effects=True,
                                              vmem_limit_bytes=VMEM_LIMIT),

time: 190 us -> 186 us (0.979)
  Pallas kernels: 189 us -> 185 us
    pallas_call x1, Pallas kernels: 166 us -> 163 us  [_main(): pl.pallas_call(_main_kernel, out_shape=(S((T, D), BF), S((T, D), BF), S((...]
where the time goes in v4:
time: 186 us
  Pallas kernels  185 us (99%)
    pallas_call x1, Pallas kernels, _main(): pl.pallas_call(_main_kernel, out_shape=(S((T, D), BF), S((T, D), BF), S((...  163 us
    pallas_call x1, Pallas kernels, _wgrad(): pl.pallas_call(_wgrad_kernel, out_shape=(S((T, D), BF), S((T, D), BF), up...  22.8 us

profile of v4, /device:TPU:0, one launch (start us, length us, event | category | flops | bytes accessed | tf_op | source)
XLA Modules:
  0.0 186.2 jit_solution(15278726227306309148)
XLA Ops:
  0.6 162.6 %moe.1 = (bf16[64,1024]{1,0:T(8,128)(2,1)}, bf16[64,1024]{1,0:T(8,128)(2,1)}, f32[128,128]{1,0:T(8,128)}, f32[1024,128]{1,0:T(8,128)}, bf16[2,8,2,64,1024]{4,3,2...) custom-call(bf16[64,1024]{1,0:T(8,128)(2,1)} %x0_ref.1, ...), custom_call_target="tpu_custom_call" | custom-call | tf_op jit(solution)/shard_map/moe/pallas_call | solution.py:439
  163.2 22.8 %wgrad.1 = (bf16[64,1024]{1,0:T(8,128)(2,1)}, bf16[64,1024]{1,0:T(8,128)(2,1)}, f32[2,1024,512]{2,1,0:T(8,128)}, f32[2,1024,512]{2,1,0:T(8,128)}, f32[2,512,1024...) custom-call(bf16[64,1024]{1,0:T(8,128)(2,1)} %get-tuple-element.29.x, ...), custom_call_target="tpu_custom_call" | custom-call | tf_op jit(solution)/shard_map/wgrad/pallas_call | solution.py:529

commit v5 on v4

--- a/solution.py
+++ b/solution.py
@@ -36,11 +36,12 @@
 
 
 def _main_kernel(x0_ref, dy_ref, ia_ref, ib_ref, ga_ref, gb_ref, w1a_h, w3a_h, w2a_h, w1b_h, w3b_h, w2b_h,
-                 x2_ref, dx0_ref, dgr_ref, gc_ref, xg_o, zg_o, h_o, da1_o, da3_o,
-                 w1, w3, w2, xg, ps, dr, ru, rd, a1s, a3s, hs, d1s, d3s, gq, gtr, dgc, dgs, tmp1, tmp3,
+                 x2_ref, dx0_ref, dgr_ref, gc_ref, xg_o, zg_o, h_o, d13_o,
+                 w13, w2, xg, ps, dr, ru, rd, a13s, hs, d13s, gq, gtr, dgc, dgs, tmp,
                  wsem, gq_s, gq_r, gx_s, gx_r, ag_s, ag_r, ax_s, ax_r, rs_s, rs_r, rx_s, rx_r, d_s, d_r, osem):
     T = x0_ref.shape[0]
     H = T // 2
+    F = w2.shape[2]
     R = 4 * T
     xin = [pltpu.make_async_copy(r, xg.at[n, OWN, 0], osem.at[n])
            for n, r in enumerate((x0_ref, dy_ref))]
@@ -55,8 +56,9 @@
 
     wcopies = []
     for l, refs in enumerate(((w1a_h, w3a_h, w2a_h), (w1b_h, w3b_h, w2b_h))):
-        for i, (src, dst) in enumerate(zip(refs, (w1, w3, w2))):
-            c = pltpu.make_async_copy(src, dst.at[l], wsem.at[l * 3 + i])
+        for i, src in enumerate(refs):
+            dst = w2.at[l] if i == 2 else w13.at[l, :, :, pl.ds(i * F, F)]
+            c = pltpu.make_async_copy(src, dst, wsem.at[l * 3 + i])
             c.start()
             wcopies.append(c)
 
@@ -84,30 +86,30 @@
     def quarter(i, q):
         return pl.ds(i * H + q * Q, Q)
 
-    pending = []
+    AGSET = (0, 1, 0, 0)
 
     AU, AD = (7, 0, 2, 4, 6), (7, 1, 3, 5, 6)
 
     def ag_u(n, j, q):
         i, h, m = j // 2, quarter(j % 2, q), 2 * j + q
-        return rcopy(xg.at[n, AU[i], 0, h], xg.at[n, AU[i + 1], 0, h], ag_s.at[n, 0, m], ag_r.at[n, 0, m], up)
+        return rcopy(xg.at[n, AU[i], 0, h], xg.at[n, AU[i + 1], 0, h], ag_s.at[AGSET[n], 0], ag_r.at[AGSET[n], 0, m], up)
 
     def ag_d(n, j, q):
         i, h, m = j // 2, quarter(1 - j % 2, q), 2 * j + q
-        return rcopy(xg.at[n, AD[i], 0, h], xg.at[n, AD[i + 1], 0, h], ag_s.at[n, 1, m], ag_r.at[n, 1, m], down)
+        return rcopy(xg.at[n, AD[i], 0, h], xg.at[n, AD[i + 1], 0, h], ag_s.at[AGSET[n], 1], ag_r.at[AGSET[n], 1, m], down)
 
     def ag_m(n, k, hf):
         return rcopy(xg.at[n, k, 0, half(hf)], xg.at[n, k, 1, half(hf)],
-                     ax_s.at[n, k * 2 + hf], ax_r.at[n, k * 2 + hf], mate)
+                     ax_s.at[AGSET[n]], ax_r.at[AGSET[n], k * 2 + hf], mate)
 
     def gq_u(h):
-        return rcopy(gq.at[AU[h], 0], gq.at[AU[h + 1], 0], gq_s.at[0, h], gq_r.at[0, h], up)
+        return rcopy(gq.at[AU[h], 0], gq.at[AU[h + 1], 0], gq_s.at[0], gq_r.at[0, h], up)
 
     def gq_d(h):
-        return rcopy(gq.at[AD[h], 0], gq.at[AD[h + 1], 0], gq_s.at[1, h], gq_r.at[1, h], down)
+        return rcopy(gq.at[AD[h], 0], gq.at[AD[h + 1], 0], gq_s.at[1], gq_r.at[1, h], down)
 
     def gq_m(k):
-        return rcopy(gq.at[k, 0], gq.at[k, 1], gx_s.at[k], gx_r.at[k], mate)
+        return rcopy(gq.at[k, 0], gq.at[k, 1], gx_s.at[0], gx_r.at[k], mate)
 
     def gq_step(h):
         def f():
@@ -168,28 +170,27 @@
                     ag_m(n, k, hf).wait_recv()
         return f
 
+    def sent(ref, sem):
+        pltpu.make_async_copy(ref, ref, sem).wait()
+
     def ag_sent(n):
-        for j in range(7):
-            for q in range(2):
-                ag_u(n, j, q).wait_send()
-                ag_d(n, j, q).wait_send()
-        for k in range(8):
-            for hf in range(2):
-                ag_m(n, k, hf).wait_send()
+        for d in range(2):
+            sent(xg.at[n, pl.ds(0, 7), 0, half(0)], ag_s.at[AGSET[n], d])
+        sent(xg.at[n, :, 0], ax_s.at[AGSET[n]])
 
     def rs_l(n, b, ch):
         return rcopy(ps.at[b, pl.ds(2 * ch, 2), 1], dr.at[b, pl.ds(2 * ch, 2)],
-                     rx_s.at[n, ch], rx_r.at[n, ch], mate)
+                     rx_s.at[b], rx_r.at[b, ch], mate)
 
     def rs_u(n, b, j, q):
         m = 2 * j + q
         return rcopy(ps.at[b, UP[(j + 1) // 2], 0, quarter(j % 2, q)], ru.at[b, j, quarter(0, q)],
-                     rs_s.at[n, 0, m], rs_r.at[n, 0, m], up)
+                     rs_s.at[b, 0], rs_r.at[b, 0, m], up)
 
     def rs_d(n, b, j, q):
         m = 2 * j + q
         return rcopy(ps.at[b, DOWN[(j + 1) // 2], 0, quarter(1 - j % 2, q)], rd.at[b, j, quarter(0, q)],
-                     rs_s.at[n, 1, m], rs_r.at[n, 1, m], down)
+                     rs_s.at[b, 1], rs_r.at[b, 1, m], down)
 
     def rs_local(n, b, *chs):
         def f():
@@ -235,12 +236,9 @@
         return f
 
     def rs_sent(n, b):
-        for j in range(7):
-            for q in range(2):
-                rs_u(n, b, j, q).wait_send()
-                rs_d(n, b, j, q).wait_send()
-        for ch in range(4):
-            rs_l(n, b, ch).wait_send()
+        for d in range(2):
+            sent(ps.at[b, pl.ds(0, 7), 0, half(0)], rs_s.at[b, d])
+        sent(ps.at[b, :, 1], rx_s.at[b])
 
     def token_loop(hooks, *stages):
         ns = len(stages)
@@ -277,23 +275,19 @@
         sg = 1.0 / (1.0 + jnp.exp(-a1))
         return sg, a1 * sg
 
-    def forward(l, n, b, ch, e, rows, a1s, a3s):
+    def forward(l, n, b, ch, e, rows, a13s):
         g = gate(l, e, rows)
-        u = rows_of(n, ch)
-        a1 = _nn(u, w1[l, e])
-        a3 = _nn(u, w3[l, e])
-        sg, sl = act(a1)
-        h = jnp.where(g >= 0, sl * a3, 0.0).astype(BF)
-        a1s[...] = a1
-        a3s[...] = a3
+        a13 = _nn(rows_of(n, ch), w13[l, e])
+        a13s[...] = a13
+        sg, sl = act(a13[:, :F])
+        h = jnp.where(g >= 0, sl * a13[:, F:], 0.0).astype(BF)
         hs[l, e, rows] = h
         put(b, ch, e, g * _nn(h, w2[l, e]).astype(BF).astype(F32))
-        return ()
-
-    def backward(l, nz, b, ch, e, rows, a1s, a3s):
+
+    def backward(l, nz, b, ch, e, rows, a13s):
         g = gate(l, e, rows)
-        a1 = a1s[...]
-        a3 = a3s[...]
+        a1 = a13s[:, :F]
+        a3 = a13s[:, F:]
         sg, sl = act(a1)
         h = hs[l, e, rows]
         r = _nt(rows_of(nz, ch), w2[l, e])
@@ -303,10 +297,9 @@
         dh = g * r
         da3 = jnp.where(g >= 0, dh * sl, 0.0).astype(BF)
         da1 = jnp.where(g >= 0, dh * a3 * sg * (1.0 + a1 * (1.0 - sg)), 0.0).astype(BF)
-        d1s[l, e, rows] = da1
-        d3s[l, e, rows] = da3
-        put(b, ch, e, (_nt(da1, w1[l, e]) + _nt(da3, w3[l, e])).astype(BF).astype(F32))
-        return ()
+        d13s[l, e, rows, 0:F] = da1
+        d13s[l, e, rows, F:2 * F] = da3
+        put(b, ch, e, _nt(d13s[l, e, rows], w13[l, e]).astype(BF).astype(F32))
 
     gq_u(0).start()
     gq_d(0).start()
@@ -323,7 +316,7 @@
         5: [gq_step(3), ag_step(0, 6), rs_local(0, 0, 1)],
         6: [rs_local(0, 0, 2), gates(3), ag_have(0, 6, 7)],
         7: [rs_merge(0, 0, 2), rs_first(0, 0), ag_step(1, 0, 1)],
-    }, lambda ch, e, rows: forward(0, 0, 0, ch, e, rows, a1s.at[e, rows], a3s.at[e, rows]))
+    }, lambda ch, e, rows: forward(0, 0, 0, ch, e, rows, a13s.at[e, rows]))
     rs_local(0, 0, 3)()
     rs_merge(0, 0, 0, 1, 3)()
     rs_second(0, 0)()
@@ -331,6 +324,7 @@
     ag_step(1, 2, 3)()
     rs_step(0, 0, 6)()
     xg[2, OWN, 0] = (xg[0, OWN, 0].astype(F32) + ps[0, OWN, 0]).astype(BF)
+    ag_sent(0)
     ag_start(2)
     rs_sent(0, 0)
     for c in wcopies[3:]:
@@ -351,8 +345,8 @@
         13: [rs_merge(2, 0, 2), rs_first(2, 0), rs_merge(2, 0, 0, 1)],
         14: [rs_local(1, 1, 3), ag_have(1, 6, 7)],
         15: [rs_merge(1, 1, 3), rs_second(1, 1)],
-    }, lambda ch, e, rows: forward(1, 2, 1, ch, e, rows, tmp1.at[e], tmp3.at[e]),
-        lambda ch, e, rows: backward(1, 1, 0, ch, e, rows, tmp1.at[e], tmp3.at[e]))
+    }, lambda ch, e, rows: forward(1, 2, 1, ch, e, rows, tmp.at[e]),
+        lambda ch, e, rows: backward(1, 1, 0, ch, e, rows, tmp.at[e]))
     rs_local(2, 0, 3)()
     outs = []
 
@@ -360,7 +354,7 @@
         c = pltpu.make_async_copy(src, dst, osem.at[i])
         c.start()
         outs.append(c)
-    for i, (sr, ds) in enumerate(((hs, h_o), (d1s, da1_o), (d3s, da3_o))):
+    for i, (sr, ds) in enumerate(((hs, h_o), (d13s, d13_o))):
         out(sr.at[1], ds.at[1], i)
     out(xg.at[0], xg_o.at[0], 3)
     out(xg.at[2], xg_o.at[1], 4)
@@ -371,6 +365,7 @@
     rs_step(1, 1, 1)()
     rs_step(2, 0, 6)()
     xg[3, OWN, 0] = (xg[1, OWN, 0].astype(F32) + ps[0, OWN, 0]).astype(BF)
+    ag_sent(2)
     ag_start(3)
     rs_sent(2, 0)
 
@@ -383,15 +378,14 @@
         5: [ag_step(3, 6), rs_step(1, 1, 3), rs_local(3, 0, 1)],
         6: [rs_local(3, 0, 2), ag_have(3, 6, 7)],
         7: [rs_merge(3, 0, 2), rs_first(3, 0)],
-    }, lambda ch, e, rows: backward(0, 3, 0, ch, e, rows, a1s.at[e, rows], a3s.at[e, rows]))
+    }, lambda ch, e, rows: backward(0, 3, 0, ch, e, rows, a13s.at[e, rows]))
     rs_local(3, 0, 3)()
     out(xg.at[3], zg_o.at[0], 6)
-    for i, (sr, ds) in enumerate(((hs, h_o), (d1s, da1_o), (d3s, da3_o))):
+    for i, (sr, ds) in enumerate(((hs, h_o), (d13s, d13_o))):
         out(sr.at[0], ds.at[0], 7 + i)
     rs_merge(3, 0, 0, 1, 3)()
     rs_second(3, 0)()
 
-    dmsgs = []
     for k in range(8):
         t = dgc[k * 2 * T:(k + 1) * 2 * T].T[0:8]
         dgs[k * 16:k * 16 + 8] = t
@@ -402,9 +396,8 @@
             if k == OWN and plane == 0:
                 continue
             dev = _ring_ep(q, core + plane * (1 - 2 * core))
-            c = rcopy(dgs.at[pl.ds(b * 8, 8)], dgr_ref.at[pl.ds(me * 8, 8)], d_s.at[b], d_r.at[b], dev)
+            c = rcopy(dgs.at[pl.ds(b * 8, 8)], dgr_ref.at[pl.ds(me * 8, 8)], d_s.at[0], d_r.at[0], dev)
             c.start()
-            dmsgs.append(c)
     dgr_ref[pl.ds(pl.multiple_of(me * 8, 8), 8)] = dgs[16 * OWN:16 * OWN + 8]
 
     rs_step(3, 0, 1, 0)()
@@ -416,11 +409,12 @@
     rs_step(3, 0, 6)()
     dx0_ref[...] = (xg[3, OWN, 0].astype(F32) + ps[0, OWN, 0]).astype(BF)
     x2_ref[...] = (xg[2, OWN, 0].astype(F32) + ps[1, OWN, 0]).astype(BF)
-    for c in dmsgs:
-        c.wait_recv()
-    for c in dmsgs + [gq_u(h) for h in range(4)] + [gq_d(h) for h in range(3)] + [gq_m(k) for k in range(8)]:
-        c.wait_send()
-    for n in range(4):
+    sent(dgs.at[pl.ds(0, 120)], d_r.at[0])
+    sent(dgs.at[pl.ds(0, 120)], d_s.at[0])
+    sent(gq.at[pl.ds(0, 4), 0], gq_s.at[0])
+    sent(gq.at[pl.ds(0, 3), 0], gq_s.at[1])
+    sent(gq.at[:, 0], gx_s.at[0])
+    for n in (1, 3):
         ag_sent(n)
     rs_sent(1, 1)
     rs_sent(3, 0)
@@ -440,23 +434,23 @@
         _main_kernel,
         out_shape=(S((T, D), BF), S((T, D), BF), S((128, 128), F32), S((N, 128), F32),
                    S((2, 8, 2, T, D), BF), S((2, 8, 2, T, D), BF),
-                   S((2, EL, N, F), BF), S((2, EL, N, F), BF), S((2, EL, N, F), BF)),
+                   S((2, EL, N, F), BF), S((2, EL, N, 2 * F), BF)),
         in_specs=[hb] * 2 + [vm] * 4 + [hb] * 6,
-        out_specs=(vm, vm, vm, vm) + (hb,) * 5,
+        out_specs=(vm, vm, vm, vm) + (hb,) * 4,
         scratch_shapes=[
-            pltpu.VMEM((2, EL, D, F), BF), pltpu.VMEM((2, EL, D, F), BF), pltpu.VMEM((2, EL, F, D), BF),
+            pltpu.VMEM((2, EL, D, 2 * F), BF), pltpu.VMEM((2, EL, F, D), BF),
             pltpu.VMEM((4, 8, 2, T, D), BF),
             pltpu.VMEM((2, 8, 2, T, D), F32), pltpu.VMEM((2, 8, T, D), F32),
             pltpu.VMEM((2, 7, T // 2, D), F32), pltpu.VMEM((2, 7, T // 2, D), F32),
-            pltpu.VMEM((EL, N, F), F32), pltpu.VMEM((EL, N, F), F32),
-            pltpu.VMEM((2, EL, N, F), BF), pltpu.VMEM((2, EL, N, F), BF), pltpu.VMEM((2, EL, N, F), BF),
+            pltpu.VMEM((EL, N, 2 * F), F32),
+            pltpu.VMEM((2, EL, N, F), BF), pltpu.VMEM((2, EL, N, 2 * F), BF),
             pltpu.VMEM((8, 2, 16, 128), F32), pltpu.VMEM((128, 128), F32), pltpu.VMEM((N, 128), F32),
             pltpu.VMEM((128, 128), F32),
-            pltpu.VMEM((EL, 4 * T, F), F32), pltpu.VMEM((EL, 4 * T, F), F32),
-            dma((6,)), dma((2, 4)), dma((2, 4)), dma((8,)), dma((8,)),
-            dma((4, 2, 14)), dma((4, 2, 14)), dma((4, 16)), dma((4, 16)),
-            dma((4, 2, 14)), dma((4, 2, 14)), dma((4, 4)), dma((4, 4)),
-            dma((16,)), dma((16,)), dma((10,)),
+            pltpu.VMEM((EL, 4 * T, 2 * F), F32),
+            dma((6,)), dma((2,)), dma((2, 4)), dma((1,)), dma((8,)),
+            dma((2, 2)), dma((2, 2, 14)), dma((2,)), dma((2, 16)),
+            dma((2, 2)), dma((2, 2, 14)), dma((2,)), dma((2, 4)),
+            dma((1,)), dma((1,)), dma((10,)),
         ],
         compiler_params=pltpu.CompilerParams(collective_id=0, has_side_effects=True,
                                              vmem_limit_bytes=VMEM_LIMIT),
@@ -468,16 +462,22 @@
     return lax.dot_general(a, b, (((0,), (0,)), ((), ())), preferred_element_type=F32)
 
 
-def _wgrad_kernel(x2_r, dx0_r, dgr, ia_ref, ib_ref, gc, xg_h, zg_h, h_h, d1_h, d3_h,
+def _wgrad_kernel(x2_r, dx0_r, dgr, ia_ref, ib_ref, gc, xg_h, zg_h, h_h, d_h,
                   x2_o, dx0_o, o1a, o3a, o2a, o1b, o3b, o2b, dga, dgb,
-                  x, z, h, d1, d3, o1, o3, o2, isem, osem):
+                  x, z, h, d, o1, o3, o2, isem, osem):
     T = x2_r.shape[0]
-    ins = []
+    F = h.shape[3]
+    def icopy(l, i, e=0):
+        if i == 1:
+            return pltpu.make_async_copy(d_h.at[l, e], d.at[l, e], isem.at[l, 1 + e])
+        src, dst, k = ((xg_h, x, 0), None, (zg_h, z, 3), (h_h, h, 4))[i]
+        return pltpu.make_async_copy(src.at[l], dst.at[l], isem.at[l, k])
     for l in (1, 0):
-        for i, (s, d) in enumerate(((xg_h, x), (d1_h, d1), (d3_h, d3), (zg_h, z), (h_h, h))):
-            c = pltpu.make_async_copy(s.at[l], d.at[l], isem.at[l, i])
-            c.start()
-            ins.append(c)
+        icopy(l, 0).start()
+        icopy(l, 1, 0).start()
+        icopy(l, 1, 1).start()
+        icopy(l, 2).start()
+        icopy(l, 3).start()
     x2_o[...] = x2_r[...]
     dx0_o[...] = dx0_r[...]
     for l, ir, o in ((0, ia_ref, dga), (1, ib_ref, dgb)):
@@ -492,18 +492,19 @@
 
     def ocopy(l, i, e):
         return pltpu.make_async_copy((o1, o3, o2)[i].at[l, e], outrefs[l][i].at[e], osem.at[l, e, i])
-    for n, l in enumerate((1, 0)):
-        for c in ins[5 * n:5 * n + 3]:
-            c.wait()
+    for l in (1, 0):
+        icopy(l, 0).wait()
 
         @pl.loop(0, 2)
         def _(e):
-            o1[l, e] = _tn(x[l], d1[l, e])
+            icopy(l, 1, e).wait()
+            v = _tn(x[l], d[l, e])
+            o1[l, e] = v[:, :F]
+            o3[l, e] = v[:, F:]
             ocopy(l, 0, e).start()
-            o3[l, e] = _tn(x[l], d3[l, e])
             ocopy(l, 1, e).start()
-        for c in ins[5 * n + 3:5 * n + 5]:
-            c.wait()
+        icopy(l, 2).wait()
+        icopy(l, 3).wait()
 
         @pl.loop(0, 2)
         def _(e):
@@ -517,7 +518,7 @@
                 ocopy(l, i, e).wait()
 
 
-def _wgrad(x2, dx0, dgr, meta, gc, xg, zg, h, d1, d3):
+def _wgrad(x2, dx0, dgr, meta, gc, xg, zg, h, d):
     T = x2.shape[0]
     _, N, D = xg.shape
     EL, F = h.shape[1], h.shape[3]
@@ -529,17 +530,17 @@
     return pl.pallas_call(
         _wgrad_kernel,
         out_shape=(S((T, D), BF), S((T, D), BF), up, up, dn, up, up, dn, S((8, T), F32), S((8, T), F32)),
-        in_specs=[vm] * 6 + [hb] * 5,
+        in_specs=[vm] * 6 + [hb] * 4,
         out_specs=(vm, vm) + (hb,) * 6 + (vm, vm),
         scratch_shapes=[
             pltpu.VMEM((2, N, D), BF), pltpu.VMEM((2, N, D), BF), pltpu.VMEM((2, EL, N, F), BF),
-            pltpu.VMEM((2, EL, N, F), BF), pltpu.VMEM((2, EL, N, F), BF),
+            pltpu.VMEM((2, EL, N, 2 * F), BF),
             pltpu.VMEM((2, EL, D, F), F32), pltpu.VMEM((2, EL, D, F), F32), pltpu.VMEM((2, EL, F, D), F32),
             dma((2, 5)), dma((2, EL, 3)),
         ],
         compiler_params=pltpu.CompilerParams(vmem_limit_bytes=VMEM_LIMIT),
         name='wgrad',
-    )(x2, dx0, dgr, *meta, gc, xg, zg, h, d1, d3)
+    )(x2, dx0, dgr, *meta, gc, xg, zg, h, d)
 
 
 def solution(mesh):
@@ -550,8 +551,8 @@
         T, D = x0.shape
         N = 16 * T
         ids = (idx_a.T, idx_b.T)
-        x2, dx0, dgr, gc, xg, zg, h, d1, d3 = _main(x0, dy, ids + (g_a.T, g_b.T), ws)
-        r = _wgrad(x2, dx0, dgr, ids, gc, xg.reshape(2, N, D), zg.reshape(2, N, D), h, d1, d3)
+        x2, dx0, dgr, gc, xg, zg, h, d = _main(x0, dy, ids + (g_a.T, g_b.T), ws)
+        r = _wgrad(x2, dx0, dgr, ids, gc, xg.reshape(2, N, D), zg.reshape(2, N, D), h, d)
         return tuple(r[:8]) + (r[8].T, r[9].T)
 
     return jax.shard_map(body, mesh=mesh,

time: 186 us -> 181 us (0.973)
  Pallas kernels: 185 us -> 180 us
    pallas_call x1, Pallas kernels: 163 us -> 158 us  [_main(): pl.pallas_call(_main_kernel, out_shape=(S((T, D), BF), S((T, D), BF), S((...]
where the time goes in v5:
time: 181 us
  Pallas kernels  180 us (99%)
    pallas_call x1, Pallas kernels, _main(): pl.pallas_call(_main_kernel, out_shape=(S((T, D), BF), S((T, D), BF), S((...  158 us
    pallas_call x1, Pallas kernels, _wgrad(): pl.pallas_call(_wgrad_kernel, out_shape=(S((T, D), BF), S((T, D), BF), up...  22.2 us

profile of v5, /device:TPU:0, one launch (start us, length us, event | category | flops | bytes accessed | tf_op | source)
XLA Modules:
  0.0 180.8 jit_solution(10700841641131638202)
XLA Ops:
  0.6 157.8 %moe.1 = (bf16[64,1024]{1,0:T(8,128)(2,1)}, bf16[64,1024]{1,0:T(8,128)(2,1)}, f32[128,128]{1,0:T(8,128)}, f32[1024,128]{1,0:T(8,128)}, bf16[2,8,2,64,1024]{4,3,2...) custom-call(bf16[64,1024]{1,0:T(8,128)(2,1)} %x0_ref.1, ...), custom_call_target="tpu_custom_call" | custom-call | tf_op jit(solution)/shard_map/moe/pallas_call | solution.py:433
  158.5 22.2 %wgrad.1 = (bf16[64,1024]{1,0:T(8,128)(2,1)}, bf16[64,1024]{1,0:T(8,128)(2,1)}, f32[2,1024,512]{2,1,0:T(8,128)}, f32[2,1024,512]{2,1,0:T(8,128)}, f32[2,512,1024...) custom-call(bf16[64,1024]{1,0:T(8,128)(2,1)} %get-tuple-element.28.x, ...), custom_call_target="tpu_custom_call" | custom-call | tf_op jit(solution)/shard_map/wgrad/pallas_call | solution.py:530

commit v6 on v5

--- a/solution.py
+++ b/solution.py
@@ -311,8 +311,8 @@
         0: [gq_step(0), ag_step(0, 0, 1), gates(0), ag_have(0, 0, 1)],
         1: [gq_step(1), ag_step(0, 2)],
         2: [ag_step(0, 3), gates(1), ag_have(0, 2, 3), rs_local(0, 0, 0)],
-        3: [gq_step(2), ag_step(0, 4)],
-        4: [ag_step(0, 5), lambda: ag_start(1), gates(2), ag_have(0, 4, 5)],
+        3: [gq_step(2), ag_step(0, 4), lambda: ag_start(1)],
+        4: [ag_step(0, 5), gates(2), ag_have(0, 4, 5)],
         5: [gq_step(3), ag_step(0, 6), rs_local(0, 0, 1)],
         6: [rs_local(0, 0, 2), gates(3), ag_have(0, 6, 7)],
         7: [rs_merge(0, 0, 2), rs_first(0, 0), ag_step(1, 0, 1)],
@@ -362,11 +362,11 @@
     rs_merge(2, 0, 3)()
     rs_second(2, 0)()
     rs_step(2, 0, 1, 0, 3, 2, 5, 4)()
-    rs_step(1, 1, 1)()
     rs_step(2, 0, 6)()
     xg[3, OWN, 0] = (xg[1, OWN, 0].astype(F32) + ps[0, OWN, 0]).astype(BF)
     ag_sent(2)
     ag_start(3)
+    rs_step(1, 1, 1)()
     rs_sent(2, 0)
 
     token_loop({
@@ -495,8 +495,7 @@
     for l in (1, 0):
         icopy(l, 0).wait()
 
-        @pl.loop(0, 2)
-        def _(e):
+        for e in range(2):
             icopy(l, 1, e).wait()
             v = _tn(x[l], d[l, e])
             o1[l, e] = v[:, :F]
@@ -506,8 +505,7 @@
         icopy(l, 2).wait()
         icopy(l, 3).wait()
 
-        @pl.loop(0, 2)
-        def _(e):
+        for e in range(2):
             g = jnp.where(e == 0, gc[:, 2 * l:2 * l + 1], gc[:, 2 * l + 1:2 * l + 2])
             do = jnp.where(g >= 0, g * z[l].astype(F32), 0.0).astype(BF)
             o2[l, e] = _tn(h[l, e], do)

time: 181 us -> 179 us (0.989)
  Pallas kernels: 180 us -> 178 us
    pallas_call x1, Pallas kernels: 22.2 us -> 20.4 us  [_wgrad(): pl.pallas_call(_wgrad_kernel, out_shape=(S((T, D), BF), S((T, D), BF), up...]
where the time goes in v6:
time: 179 us
  Pallas kernels  178 us (99%)
    pallas_call x1, Pallas kernels, _main(): pl.pallas_call(_main_kernel, out_shape=(S((T, D), BF), S((T, D), BF), S((...  158 us
    pallas_call x1, Pallas kernels, _wgrad(): pl.pallas_call(_wgrad_kernel, out_shape=(S((T, D), BF), S((T, D), BF), up...  20.4 us

profile of v6, /device:TPU:0, one launch (start us, length us, event | category | flops | bytes accessed | tf_op | source)
XLA Modules:
  0.0 178.8 jit_solution(11249906775801506768)
XLA Ops:
  0.6 157.6 %moe.1 = (bf16[64,1024]{1,0:T(8,128)(2,1)}, bf16[64,1024]{1,0:T(8,128)(2,1)}, f32[128,128]{1,0:T(8,128)}, f32[1024,128]{1,0:T(8,128)}, bf16[2,8,2,64,1024]{4,3,2...) custom-call(bf16[64,1024]{1,0:T(8,128)(2,1)} %x0_ref.1, ...), custom_call_target="tpu_custom_call" | custom-call | tf_op jit(solution)/shard_map/moe/pallas_call | solution.py:433
  158.3 20.4 %wgrad.1 = (bf16[64,1024]{1,0:T(8,128)(2,1)}, bf16[64,1024]{1,0:T(8,128)(2,1)}, f32[2,1024,512]{2,1,0:T(8,128)}, f32[2,1024,512]{2,1,0:T(8,128)}, f32[2,512,1024...) custom-call(bf16[64,1024]{1,0:T(8,128)(2,1)} %get-tuple-element.28.x, ...), custom_call_target="tpu_custom_call" | custom-call | tf_op jit(solution)/shard_map/wgrad/pallas_call | solution.py:528

commit v7 on v6

--- a/solution.py
+++ b/solution.py
@@ -261,7 +261,27 @@
                     def _():
                         stages[k](ch, e, rows)
 
+    def pair_loop(hooks, *stages):
+        ns = len(stages)
+
+        @pl.loop(0, 4 * ns)
+        def _(it):
+            for i, fs in hooks.items():
+                @pl.when(it == i)
+                def _():
+                    for f in fs:
+                        f()
+            ch = it // ns
+            rows = pl.ds(pl.multiple_of(ch * R, R), R)
+            for k in range(ns):
+                @pl.when(it % ns == k)
+                def _():
+                    for e in range(2):
+                        stages[k](ch, e, rows)
+
     def gate(l, e, rows):
+        if isinstance(e, int):
+            return gc_ref[rows, 2 * l + e:2 * l + e + 1]
         return jnp.where(e == 0, gc_ref[rows, 2 * l:2 * l + 1], gc_ref[rows, 2 * l + 1:2 * l + 2])
 
     def rows_of(n, ch):
@@ -269,7 +289,11 @@
 
     def put(b, ch, e, v):
         s = pl.ds(2 * ch, 2)
-        ps[b, s] = jnp.where(e == 0, 0.0, ps[b, s]) + v.reshape(2, 2, T, v.shape[-1])
+        v = v.reshape(2, 2, T, v.shape[-1])
+        if isinstance(e, int):
+            ps[b, s] = v if e == 0 else ps[b, s] + v
+        else:
+            ps[b, s] = jnp.where(e == 0, 0.0, ps[b, s]) + v
 
     def act(a1):
         sg = 1.0 / (1.0 + jnp.exp(-a1))
@@ -330,21 +354,15 @@
     for c in wcopies[3:]:
         c.wait()
 
-    token_loop({
+    pair_loop({
         0: [ag_step(2, 0, 1), ag_have(2, 0, 1)],
-        1: [ag_step(2, 2), ag_step(1, 4)],
-        2: [ag_step(2, 3), ag_step(1, 5), ag_have(1, 0, 1)],
-        3: [ag_step(2, 4), ag_step(1, 6)],
-        4: [ag_step(2, 5), ag_have(2, 2, 3), rs_local(2, 0, 0), rs_local(1, 1, 0)],
-        5: [ag_step(2, 6)],
-        6: [ag_have(1, 2, 3)],
-        8: [ag_have(2, 4, 5), rs_local(2, 0, 1), rs_local(1, 1, 1)],
-        10: [rs_local(1, 1, 2), ag_have(1, 4, 5), rs_merge(1, 1, 0, 1)],
-        11: [rs_merge(1, 1, 2), rs_first(1, 1)],
-        12: [rs_local(2, 0, 2), ag_have(2, 6, 7)],
-        13: [rs_merge(2, 0, 2), rs_first(2, 0), rs_merge(2, 0, 0, 1)],
-        14: [rs_local(1, 1, 3), ag_have(1, 6, 7)],
-        15: [rs_merge(1, 1, 3), rs_second(1, 1)],
+        1: [ag_step(2, 2, 3), ag_step(1, 4, 5), ag_have(1, 0, 1)],
+        2: [ag_step(2, 4), ag_step(1, 6), ag_have(2, 2, 3), rs_local(2, 0, 0), rs_local(1, 1, 0)],
+        3: [ag_step(2, 5, 6), ag_have(1, 2, 3)],
+        4: [ag_have(2, 4, 5), rs_local(2, 0, 1), rs_local(1, 1, 1)],
+        5: [rs_local(1, 1, 2), ag_have(1, 4, 5), rs_merge(1, 1, 0, 1, 2), rs_first(1, 1)],
+        6: [rs_local(2, 0, 2), ag_have(2, 6, 7), rs_merge(2, 0, 0, 1)],
+        7: [rs_merge(2, 0, 2), rs_first(2, 0), rs_local(1, 1, 3), ag_have(1, 6, 7), rs_merge(1, 1, 3), rs_second(1, 1)],
     }, lambda ch, e, rows: forward(1, 2, 1, ch, e, rows, tmp.at[e]),
         lambda ch, e, rows: backward(1, 1, 0, ch, e, rows, tmp.at[e]))
     rs_local(2, 0, 3)()

time: 179 us -> 179 us (level)
  no operation moved by 1% of the time
where the time goes in v7:
time: 179 us
  Pallas kernels  178 us (99%)
    pallas_call x1, Pallas kernels, _main(): pl.pallas_call(_main_kernel, out_shape=(S((T, D), BF), S((T, D), BF), S((...  158 us
    pallas_call x1, Pallas kernels, _wgrad(): pl.pallas_call(_wgrad_kernel, out_shape=(S((T, D), BF), S((T, D), BF), up...  20.4 us

profile of v7, /device:TPU:0, one launch (start us, length us, event | category | flops | bytes accessed | tf_op | source)
XLA Modules:
  0.0 179.1 jit_solution(8527681267973752999)
XLA Ops:
  0.6 158.0 %moe.1 = (bf16[64,1024]{1,0:T(8,128)(2,1)}, bf16[64,1024]{1,0:T(8,128)(2,1)}, f32[128,128]{1,0:T(8,128)}, f32[1024,128]{1,0:T(8,128)}, bf16[2,8,2,64,1024]{4,3,2...) custom-call(bf16[64,1024]{1,0:T(8,128)(2,1)} %x0_ref.1, ...), custom_call_target="tpu_custom_call" | custom-call | tf_op jit(solution)/shard_map/moe/pallas_call | solution.py:451
  158.6 20.4 %wgrad.1 = (bf16[64,1024]{1,0:T(8,128)(2,1)}, bf16[64,1024]{1,0:T(8,128)(2,1)}, f32[2,1024,512]{2,1,0:T(8,128)}, f32[2,1024,512]{2,1,0:T(8,128)}, f32[2,512,1024...) custom-call(bf16[64,1024]{1,0:T(8,128)(2,1)} %get-tuple-element.28.x, ...), custom_call_target="tpu_custom_call" | custom-call | tf_op jit(solution)/shard_map/wgrad/pallas_call | solution.py:546
